TPU v7x, 128 devices: a whole 4x4x4 slice. The times are simulated.
128 devices in a mesh: pts: 128 (over y, x, z, core).
Axes of the slice: x: 4, y: 4, z: 4, core: 2. Of those that a mesh axis runs over, the one named last changes fastest.
Arguments:
- point_data: float32 [5, 131072], P(None, 'pts'), may hold values from -1 to 1
- point_counts: int32 [128], P('pts'), may hold values from 64 to 1024, as said below
- point_offsets: int32 [128], P('pts'), may hold values from 0 to 960, as said below
- in_weight: float32 [3, 256], replicated, may hold values from -6 to 6
- input_bias: float32 [256], replicated, may hold values from -3 to 3
- hidden_layer_weight: float32 [3, 256, 256], replicated, may hold values from -0.5 to 0.5
- hidden_bias: float32 [3, 256], replicated, may hold values from -3 to 3
- output_weight: float32 [3, 256], replicated, may hold values from -0.75 to 0.75
- out_bias: float32 [3], replicated, may hold values from -3 to 3
Outputs:
- grad_in_weight: float32 [3, 256], replicated
- grad_in_bias: float32 [256], replicated
- grad_hidden_weight: float32 [3, 256, 256], replicated
- grad_hidden_bias: float32 [3, 256], replicated
- grad_out_weight: float32 [3, 256], replicated
- grad_out_bias: float32 [3], replicated
- term_means: float32 [3], replicated
Inputs may be any that keep to these rules, and one draw needn't show every extreme that they name: `point_counts`: some device has exactly 1024 live points and another exactly 64. A device's live points fill its slots point_offsets to point_offsets + point_counts - 1, all within its 1024 slots.
All inputs are finite; a program needn't handle non-finite values.
Results may differ from a plain program's by a relative error of at most 0.0001.
Values sent between devices are 32-bit elements; how exact they have to be, the bound alone decides.
No kernel may reach another device: no remote copies, remote signals or barrier semaphores. Data moves between devices by JAX's collectives and lax.ppermute only.
A program may use at most 64 MiB of HBM per device.

v0:
```python
import jax
import jax.numpy as jnp
from jax import lax
from jax.sharding import Mesh
from jax.sharding import PartitionSpec as P

BLOCK = 256
PTS = ("pts_0", "pts_1", "pts_2", "pts_3")


viscosity = 0.2
term_weights = (2.0, 1.0, 1.0)
highest_precision = lax.Precision.HIGHEST


def padded_to(lines, count):
    spare = -lines.shape[0] % count
    if not spare:
        return lines
    return jnp.concatenate([lines, jnp.zeros((spare, *lines.shape[1:]), lines.dtype)])


def sent_to_all(value, axis):
    count = lax.axis_size(axis)
    return lax.all_to_all(
        jnp.broadcast_to(value[None], (count, *value.shape)), axis, 0, 0, tiled=True
    )


def joined_along(parts, dim):
    shape = list(parts.shape[1:])
    shape[dim] *= parts.shape[0]
    return jnp.moveaxis(parts, 0, dim).reshape(shape)


def gathered_by_axis(value, axes, dim):
    far, near = axes
    first = sent_to_all(value, far)
    parts = jnp.swapaxes(sent_to_all(first, near), 0, 1)
    return joined_along(parts.reshape(-1, *value.shape), dim)


def in_blocks(value, dim, count):
    shape = value.shape
    parts = value.reshape(*shape[:dim], count, shape[dim] // count, *shape[dim + 1 :])
    return jnp.moveaxis(parts, dim, 0)


def summed_on_arrival(value, axis, dim):
    parts = in_blocks(value, dim, lax.axis_size(axis))
    arrived = lax.all_to_all(parts, axis, split_axis=0, concat_axis=0, tiled=True)
    return arrived.sum(axis=0)


def summed_rows(value, axes, dim):
    far, near = axes
    own = summed_on_arrival(in_blocks(value, dim, lax.axis_size(far)), near, dim + 1)
    return jnp.sum(lax.all_to_all(own, far, 0, 0, tiled=True), axis=0)


def nested_sum(value, axes):
    padded = padded_to(value, lax.axis_size(axes[0]) * lax.axis_size(axes[1]))
    whole = gathered_by_axis(summed_rows(padded, axes, 0), axes, 0)
    return lax.slice_in_dim(whole, 0, len(value)).reshape(value.shape)


def packed_total(arrays, axis):
    ravelled, at, outs = (jnp.concatenate([a.reshape(-1) for a in arrays]), 0, [])
    total = nested_sum(ravelled, axis)
    for a in arrays:
        outs.append(total[at : at + a.size].reshape(a.shape))
        at += a.size
    return tuple(outs)


def apply_tanh(stack_arrays):
    hidden = jnp.tanh(stack_arrays[0])
    slope = 1.0 - hidden * hidden
    firsts = slope[None] * stack_arrays[1:4]
    seconds = (
        slope[None] * stack_arrays[4:6]
        - 2.0 * (hidden * slope)[None] * stack_arrays[1:3] * stack_arrays[1:3]
    )
    return jnp.concatenate([hidden[None], firsts, seconds], 0)


def add_bias(stack_arrays, bias):
    return jnp.concatenate([stack_arrays[0:1] + bias[None, :, None], stack_arrays[1:]], 0)


def network_jets(params, coords):
    in_weight, input_bias, hidden_layer_weight, hidden_bias, output_weight, out_bias = params
    rows = coords.shape[1]
    value = (
        jnp.dot(
            in_weight.T, coords, precision=highest_precision, preferred_element_type=jnp.float32
        )
        + input_bias[:, None]
    )
    firsts = in_weight[:, :, None] * jnp.ones((1, 1, rows), jnp.float32)
    zeros = jnp.zeros((2,) + value.shape, jnp.float32)
    stack_arrays = jnp.concatenate([value[None], firsts, zeros], 0)
    for layer_apply in range(hidden_layer_weight.shape[0]):
        stack_arrays = jnp.einsum(
            "hm,xmj->xhj",
            hidden_layer_weight[layer_apply],
            apply_tanh(stack_arrays),
            precision=highest_precision,
        )
        stack_arrays = add_bias(stack_arrays, hidden_bias[layer_apply])
    stack_arrays = jnp.einsum(
        "hm,xmj->xhj", output_weight, apply_tanh(stack_arrays), precision=highest_precision
    )
    return add_bias(stack_arrays, out_bias)


def residual_totals(params, block_data, mask):
    out = network_jets(params, block_data[0:3])
    x_vel, y_vel = (out[0, 0], out[0, 1])
    continuity = out[1, 0] + out[2, 1]
    momentum_x = (
        out[3, 0]
        + x_vel * out[1, 0]
        + y_vel * out[2, 0]
        + out[1, 2]
        - viscosity * (out[4, 0] + out[5, 0])
        - block_data[3]
    )
    momentum_y = (
        out[3, 1]
        + x_vel * out[1, 1]
        + y_vel * out[2, 1]
        + out[2, 2]
        - viscosity * (out[4, 1] + out[5, 1])
        - block_data[4]
    )
    return jnp.stack(
        [
            jnp.sum(mask * continuity * continuity),
            jnp.sum(mask * momentum_x * momentum_x),
            jnp.sum(mask * momentum_y * momentum_y),
        ]
    )


def shards(
    point_data,
    point_counts,
    point_offsets,
    in_weight,
    input_bias,
    hidden_layer_weight,
    hidden_bias,
    output_weight,
    out_bias,
):
    params = (in_weight, input_bias, hidden_layer_weight, hidden_bias, output_weight, out_bias)
    live_count = point_counts[0]
    live_start = point_offsets[0]
    weights = jnp.array(term_weights, jnp.float32)
    first_block = live_start // BLOCK
    end_block = (live_start + live_count + BLOCK - 1) // BLOCK

    def step(index, carry):
        sums, grads = carry
        block_data = lax.dynamic_slice_in_dim(point_data, index * BLOCK, BLOCK, 1)
        slots = index * BLOCK + jnp.arange(BLOCK, dtype=jnp.int32)
        mask = ((slots >= live_start) & (slots < live_start + live_count)).astype(jnp.float32)
        block_sums, pullback = jax.vjp(lambda p: residual_totals(p, block_data, mask), params)
        block_grads = pullback(weights)[0]
        return (sums + block_sums, jax.tree.map(jnp.add, grads, block_grads))

    start = (jnp.zeros((3,), jnp.float32), jax.tree.map(jnp.zeros_like, params))
    sums, grads = lax.fori_loop(first_block, end_block, step, start)
    own_count = point_counts.astype(jnp.float32)
    reduced = packed_total(
        (grads[0], grads[1], grads[2], grads[3], grads[4], grads[5], sums, own_count),
        (("pts_0", "pts_1", "pts_2"), "pts_3"),
    )
    total = reduced[7][0]
    return (
        reduced[0] / total,
        reduced[1] / total,
        reduced[2] / total,
        reduced[3] / total,
        reduced[4] / total,
        reduced[5] / total,
        reduced[6] / total,
    )


def solution(mesh):
    torus = Mesh(mesh.devices.reshape(4, 4, 4, 2), ("pts_0", "pts_1", "pts_2", "pts_3"))
    placed = (P(None, PTS), P(PTS), P(PTS), P(), P(), P(), P(), P(), P())
    return jax.shard_map(
        shards,
        mesh=torus,
        in_specs=placed,
        out_specs=(P(), P(), P(), P(), P(), P(), P()),
        check_vma=False,
    )
```

profile of v0, /device:TPU:1, one launch (start us, length us, event | category | flops | bytes accessed | tf_op | source)
XLA Modules:
  0.0 212.4 jit_solution(1076998236131349949)
XLA Ops:
  2.1 111.6 %while.25 = (s32[]{:T(128)}, f32[3]{0:T(128)S(1)}, f32[3,256]{1,0:T(4,128)S(1)}, f32[256]{0:T(256)S(1)}, f32[3,256,256]{2,1,0:T(8,128)S(1)}, /*index=5*/f32[3,25...) while((s32[]{:T(128)}, f32[3]{0:T(128)S(1)}, ...), condition=%wide.region_22.23_spmd.clone, body=%wide.region_0.22_spmd.sunk.clone.sunk | while | flops 10953214976 | bytes 130055376 | solution.py:174
  2.9 0.8 fusion.184
  3.7 1.2 fusion.182
  5.1 1.5 convolution_bitcast_fusion.10
  6.9 1.5 convolution_bitcast_fusion.11
  8.6 1.5 convolution_bitcast_fusion.12
  10.9 1.4 convolution_bitcast_fusion.13
  12.4 1.4 negate_multiply_fusion.5
  13.8 1.4 negate_multiply_fusion.4
  15.9 1.3 fusion.191
  17.2 2.0 maximum_add_fusion.2
  19.4 0.8 fusion.204
  20.2 1.7 convolution_bitcast_fusion.14
  22.7 2.8 %fusion.203 = f32[1,256,256]{2,1,0:T(8,128)S(1)} fusion(f32[2,256,256]{1,2,0:T(8,128)S(1)} %fusion.188, f32[3,256,256]{1,2,0:T(8,128)S(1)} %slice_multiply_fusion.24, f32[1,256,256]{1,2,0:T(8,128)S(1)} %get-tuple-element.596, f32[6,256,256]{1,2,0:T(8,128)S(1)} %pad_add_fusion.15, f32[5,256,256]{1,2,0:T(8,128)S(1)} %split.277, ...), kind=kOutput, calls=%fused_computation.30.clone.1 | convolution fusion | flops 1209532416 | bytes 4718598 | tf_op jit(solution)/shard_map/while/body/transpose(jvp(hm,xmj->xhj))/dot_general | solution.py:104
  25.5 1.5 fusion.193
  27.8 2.8 %fusion.202 = f32[1,256,256]{2,1,0:T(8,128)S(1)} fusion(f32[2,256,256]{1,2,0:T(8,128)S(1)} %fusion.186, f32[3,256,256]{1,2,0:T(8,128)S(1)} %slice_multiply_fusion.23, f32[1,256,256]{1,2,0:T(8,128)S(1)} %get-tuple-element.593, f32[6,256,256]{1,2,0:T(8,128)S(1)} %pad_add_fusion.16, f32[5,256,256]{1,2,0:T(8,128)S(1)} %split.278, ...), kind=kOutput, calls=%fused_computation.31.clone.1 | convolution fusion | flops 1209532416 | bytes 4718598 | tf_op jit(solution)/shard_map/while/body/transpose(jvp(hm,xmj->xhj))/dot_general | solution.py:104
  30.6 1.5 fusion.195
  33.0 2.8 %fusion.201 = f32[1,256,256]{2,1,0:T(8,128)S(1)} fusion(f32[2,256,256]{1,2,0:T(8,128)S(1)} %fusion.183, f32[3,256,256]{1,2,0:T(8,128)S(1)} %broadcast_multiply_fusion.3, f32[1,256,256]{1,2,0:T(8,128)S(1)} %bitcast.373, f32[6,256,256]{1,2,0:T(8,128)S(1)} %pad_add_fusion.17, f32[5,256,256]{1,2,0:T(8,128)S(1)} %split.279, pred[6]{0:T(512)(128)(4,1)S(1)} %copy-done.2), kind=kOutput, calls=%fused_computation.32.clone.1 | convolution fusion | flops 1209532416 | bytes 4718598 | tf_op jit(solution)/shard_map/while/body/transpose(jvp(hm,xmj->xhj))/dot_general | solution.py:104
  35.8 1.5 fusion.197
  38.3 0.9 fusion.200
  40.0 0.8 fusion.184
  40.8 1.2 fusion.182
  42.2 1.5 convolution_bitcast_fusion.10
  44.0 1.5 convolution_bitcast_fusion.11
  45.8 1.5 convolution_bitcast_fusion.12
  48.0 1.4 convolution_bitcast_fusion.13
  49.5 1.4 negate_multiply_fusion.5
  51.0 1.4 negate_multiply_fusion.4
  53.1 1.3 fusion.191
  54.3 2.0 maximum_add_fusion.2
  57.3 1.7 convolution_bitcast_fusion.14
  59.8 2.8 %fusion.203 = f32[1,256,256]{2,1,0:T(8,128)S(1)} fusion(f32[2,256,256]{1,2,0:T(8,128)S(1)} %fusion.188, f32[3,256,256]{1,2,0:T(8,128)S(1)} %slice_multiply_fusion.24, f32[1,256,256]{1,2,0:T(8,128)S(1)} %get-tuple-element.596, f32[6,256,256]{1,2,0:T(8,128)S(1)} %pad_add_fusion.15, f32[5,256,256]{1,2,0:T(8,128)S(1)} %split.277, ...), kind=kOutput, calls=%fused_computation.30.clone.1 | convolution fusion | flops 1209532416 | bytes 4718598 | tf_op jit(solution)/shard_map/while/body/transpose(jvp(hm,xmj->xhj))/dot_general | solution.py:104
  62.6 1.5 fusion.193
  65.0 2.8 %fusion.202 = f32[1,256,256]{2,1,0:T(8,128)S(1)} fusion(f32[2,256,256]{1,2,0:T(8,128)S(1)} %fusion.186, f32[3,256,256]{1,2,0:T(8,128)S(1)} %slice_multiply_fusion.23, f32[1,256,256]{1,2,0:T(8,128)S(1)} %get-tuple-element.593, f32[6,256,256]{1,2,0:T(8,128)S(1)} %pad_add_fusion.16, f32[5,256,256]{1,2,0:T(8,128)S(1)} %split.278, ...), kind=kOutput, calls=%fused_computation.31.clone.1 | convolution fusion | flops 1209532416 | bytes 4718598 | tf_op jit(solution)/shard_map/while/body/transpose(jvp(hm,xmj->xhj))/dot_general | solution.py:104
  67.8 1.5 fusion.195
  70.2 2.8 %fusion.201 = f32[1,256,256]{2,1,0:T(8,128)S(1)} fusion(f32[2,256,256]{1,2,0:T(8,128)S(1)} %fusion.183, f32[3,256,256]{1,2,0:T(8,128)S(1)} %broadcast_multiply_fusion.3, f32[1,256,256]{1,2,0:T(8,128)S(1)} %bitcast.373, f32[6,256,256]{1,2,0:T(8,128)S(1)} %pad_add_fusion.17, f32[5,256,256]{1,2,0:T(8,128)S(1)} %split.279, pred[6]{0:T(512)(128)(4,1)S(1)} %copy-done.2), kind=kOutput, calls=%fused_computation.32.clone.1 | convolution fusion | flops 1209532416 | bytes 4718598 | tf_op jit(solution)/shard_map/while/body/transpose(jvp(hm,xmj->xhj))/dot_general | solution.py:104
  73.0 1.5 fusion.197
  75.4 0.9 fusion.200
  77.2 0.8 fusion.184
  78.0 1.2 fusion.182
  79.4 1.5 convolution_bitcast_fusion.10
  81.1 1.5 convolution_bitcast_fusion.11
  82.9 1.5 convolution_bitcast_fusion.12
  85.2 1.4 convolution_bitcast_fusion.13
  86.7 1.4 negate_multiply_fusion.5
  88.1 1.4 negate_multiply_fusion.4
  90.2 1.3 fusion.191
  91.5 2.0 maximum_add_fusion.2
  94.4 1.7 convolution_bitcast_fusion.14
  97.0 2.8 %fusion.203 = f32[1,256,256]{2,1,0:T(8,128)S(1)} fusion(f32[2,256,256]{1,2,0:T(8,128)S(1)} %fusion.188, f32[3,256,256]{1,2,0:T(8,128)S(1)} %slice_multiply_fusion.24, f32[1,256,256]{1,2,0:T(8,128)S(1)} %get-tuple-element.596, f32[6,256,256]{1,2,0:T(8,128)S(1)} %pad_add_fusion.15, f32[5,256,256]{1,2,0:T(8,128)S(1)} %split.277, ...), kind=kOutput, calls=%fused_computation.30.clone.1 | convolution fusion | flops 1209532416 | bytes 4718598 | tf_op jit(solution)/shard_map/while/body/transpose(jvp(hm,xmj->xhj))/dot_general | solution.py:104
  99.8 1.5 fusion.193
  102.1 2.8 %fusion.202 = f32[1,256,256]{2,1,0:T(8,128)S(1)} fusion(f32[2,256,256]{1,2,0:T(8,128)S(1)} %fusion.186, f32[3,256,256]{1,2,0:T(8,128)S(1)} %slice_multiply_fusion.23, f32[1,256,256]{1,2,0:T(8,128)S(1)} %get-tuple-element.593, f32[6,256,256]{1,2,0:T(8,128)S(1)} %pad_add_fusion.16, f32[5,256,256]{1,2,0:T(8,128)S(1)} %split.278, ...), kind=kOutput, calls=%fused_computation.31.clone.1 | convolution fusion | flops 1209532416 | bytes 4718598 | tf_op jit(solution)/shard_map/while/body/transpose(jvp(hm,xmj->xhj))/dot_general | solution.py:104
  104.9 1.5 fusion.195
  107.3 2.8 %fusion.201 = f32[1,256,256]{2,1,0:T(8,128)S(1)} fusion(f32[2,256,256]{1,2,0:T(8,128)S(1)} %fusion.183, f32[3,256,256]{1,2,0:T(8,128)S(1)} %broadcast_multiply_fusion.3, f32[1,256,256]{1,2,0:T(8,128)S(1)} %bitcast.373, f32[6,256,256]{1,2,0:T(8,128)S(1)} %pad_add_fusion.17, f32[5,256,256]{1,2,0:T(8,128)S(1)} %split.279, pred[6]{0:T(512)(128)(4,1)S(1)} %copy-done.2), kind=kOutput, calls=%fused_computation.32.clone.1 | convolution fusion | flops 1209532416 | bytes 4718598 | tf_op jit(solution)/shard_map/while/body/transpose(jvp(hm,xmj->xhj))/dot_general | solution.py:104
  110.1 1.5 fusion.197
  112.6 0.9 fusion.200
  114.9 1.0 reshape_reshape.6
  115.9 5.4 %all_to_all.27 = f32[2,64,1557]{2,1,0:T(8,128)S(1)} all-to-all(f32[2,64,1557]{2,1,0:T(8,128)S(1)} %copy.50), channel_id=1, replica_groups=mesh['pts_0'=4,'pts_1'=4,'pts_2'=4,'pts_3'=2] {'pts_3'}, dimensions={0} | all-to-all | bytes 1594368 | tf_op jit(solution)/shard_map/all_to_all | solution.py:51
  121.7 59.4 %all_to_all.28 = f32[64,1,1557]{2,1,0:T(1,128)S(1)} all-to-all(f32[64,1,1557]{2,1,0:T(1,128)S(1)} %all_to_all.17), channel_id=1, replica_groups=mesh['pts_0'=4,'pts_1'=4,'pts_2'=4,'pts_3'=2] {'pts_0','pts_1','pts_2'}, dimensions={0} | all-to-all | bytes 797184 | tf_op jit(solution)/shard_map/all_to_all | solution.py:58
  181.6 14.8 %all_to_all.25 = f32[64,1,1557]{2,1,0:T(1,128)S(1)} all-to-all(f32[64,1,1557]{2,1,0:T(1,128)S(1)} %broadcast_in_dim.101), channel_id=1, replica_groups=mesh['pts_0'=4,'pts_1'=4,'pts_2'=4,'pts_3'=2] {'pts_0','pts_1','pts_2'}, dimensions={0} | all-to-all | bytes 797184 | tf_op jit(solution)/shard_map/all_to_all | solution.py:25
  196.5 7.2 %all_to_all.26 = f32[2,64,1557]{2,1,0:T(8,128)S(1)} all-to-all(f32[2,64,1557]{2,1,0:T(8,128)S(1)} %broadcast_in_dim.103), channel_id=1, replica_groups=mesh['pts_0'=4,'pts_1'=4,'pts_2'=4,'pts_3'=2] {'pts_3'}, dimensions={0} | all-to-all | bytes 1594368 | tf_op jit(solution)/shard_map/all_to_all | solution.py:25
  205.7 1.2 slice_divide_fusion.4
  206.9 1.2 slice_divide_fusion.5
  209.5 1.1 div.76
  (204 shorter events, 28.3 us)
Async XLA Ops:
  2.1 2.9 %copy-start.1 = (f32[3,256]{1,0:T(4,128)S(1)}, f32[3,256]{1,0:T(4,128)}, u32[]{:S(2)}) copy-start(f32[3,256]{1,0:T(4,128)} %get-tuple-element.712) | copy-start | bytes 9220 | tf_op jit(solution)/shard_map/while
  3.7 1.4 copy-start
  10.2 0.7 copy-start.3
  10.3 2.0 copy-start.4
  10.4 9.0 %copy-start.2 = (pred[6]{0:T(512)(128)(4,1)S(1)}, pred[6]{0:T(512)(128)(4,1)}, u32[]{:S(2)}) copy-start(pred[6]{0:T(512)(128)(4,1)} %get-tuple-element.724) | copy-start | bytes 22 | tf_op jit(solution)/shard_map/while
  39.3 2.9 %copy-start.1 = (f32[3,256]{1,0:T(4,128)S(1)}, f32[3,256]{1,0:T(4,128)}, u32[]{:S(2)}) copy-start(f32[3,256]{1,0:T(4,128)} %get-tuple-element.712) | copy-start | bytes 9220 | tf_op jit(solution)/shard_map/while
  40.8 1.4 copy-start
  47.4 0.7 copy-start.3
  47.5 2.0 copy-start.4
  47.5 9.0 %copy-start.2 = (pred[6]{0:T(512)(128)(4,1)S(1)}, pred[6]{0:T(512)(128)(4,1)}, u32[]{:S(2)}) copy-start(pred[6]{0:T(512)(128)(4,1)} %get-tuple-element.724) | copy-start | bytes 22 | tf_op jit(solution)/shard_map/while
  76.4 2.9 %copy-start.1 = (f32[3,256]{1,0:T(4,128)S(1)}, f32[3,256]{1,0:T(4,128)}, u32[]{:S(2)}) copy-start(f32[3,256]{1,0:T(4,128)} %get-tuple-element.712) | copy-start | bytes 9220 | tf_op jit(solution)/shard_map/while
  78.0 1.4 copy-start
  84.5 0.7 copy-start.3
  84.6 2.0 copy-start.4
  84.6 9.0 %copy-start.2 = (pred[6]{0:T(512)(128)(4,1)S(1)}, pred[6]{0:T(512)(128)(4,1)}, u32[]{:S(2)}) copy-start(pred[6]{0:T(512)(128)(4,1)} %get-tuple-element.724) | copy-start | bytes 22 | tf_op jit(solution)/shard_map/while
where the time goes:
time: 214 us; the launch traced here: 212 us
  blocking collectives  86.9 us (41%)
  matrix products  69.7 us (33%)
  other arithmetic  37.4 us (17%)
  local copies, waits for them, and re-layouts  14.6 us (7%)
    all_to_all x1, blocking collectives, summed_rows(): return jnp.sum(lax.all_to_all(own, far, 0, 0, tiled=True), axis=0)  59.4 us
    dot_general x27, matrix products, network_jets(): jnp.einsum('hm,xmj->xhj', hidden_layer_weight[layer_apply], apply_tanh(st...  51.7 us
    all_to_all x2, blocking collectives, sent_to_all(): lax.all_to_all(jnp.broadcast_to(value[None], (count, *value.shape)), axis...  22 us
    dot_general x9, matrix products, network_jets(): jnp.einsum('hm,xmj->xhj', output_weight, apply_tanh(stack_arrays), precis...  11.6 us
    add x15, other arithmetic, step(): return (sums + block_sums, jax.tree.map(jnp.add, grads, block_grads))  6.78 us
    dot_general x6, matrix products, network_jets(): jnp.dot(in_weight.T, coords, precision=highest_precision, preferred_eleme...  6.41 us
    all_to_all x1, blocking collectives, summed_on_arrival(): lax.all_to_all(parts, axis, split_axis=0, concat_axis=0, tiled=True)  5.44 us
    mul x3, other arithmetic, residual_totals(): viscosity * (out[4, 0] + out[5, 0])  4.33 us

commit v1 on v0

v1 whole, which is shorter than its diff:
```python
import functools

import jax
import jax.numpy as jnp
from jax import lax
from jax.experimental import pallas as pl
from jax.experimental.pallas import tpu as pltpu
from jax.sharding import Mesh
from jax.sharding import PartitionSpec as P

PTS = ("pts_0", "pts_1", "pts_2", "pts_3")
FAR = ("pts_0", "pts_1", "pts_2")
NEAR = "pts_3"

VISCOSITY = 0.2
BLOCK = 256
WIDTH = 256
ROWS = 16
CHUNKS = WIDTH // ROWS
F32 = jnp.float32
BF16 = jnp.bfloat16
JETS = 5
SMALL_ROW = 3 * 512
PACKED_ROWS = 1664


def split(x):
    high = x.astype(BF16)
    return high, (x - high.astype(F32)).astype(BF16)


def matmul(a, b):
    return lax.dot_general(a, b, (((1,), (0,)), ((), ())), preferred_element_type=F32)


def matmul_nt(a, b):
    return lax.dot_general(a, b, (((1,), (1,)), ((), ())), preferred_element_type=F32)


def fold(x):
    return x[:, :128] + x[:, 128:]


def step_kernel(
    counts_ref,
    offsets_ref,
    data_ref,
    in_w_ref,
    in_b_ref,
    hid_w_ref,
    hid_b_ref,
    out_w_ref,
    out_b_ref,
    packed_ref,
    w_cat,
    wt_cat,
    w0_cat,
    wt0_cat,
    out_cat,
    cols,
    z_buf,
    h_buf,
    s_buf,
    q_buf,
    ah_buf,
    al_buf,
    a0h_buf,
    a0l_buf,
    a3_buf,
    g_buf,
    dzh_buf,
    dzl_buf,
    grad_w,
    grad_g,
    partial,
    sums_buf,
):
    live_start = offsets_ref[0]
    live_count = counts_ref[0]
    first_block = live_start // BLOCK
    end_block = (live_start + live_count + BLOCK - 1) // BLOCK

    def put_cat(ref, index, value):
        high, low = split(value)
        ref[index, :, 0:256] = high
        ref[index, :, 256:512] = low
        ref[index, :, 512:768] = high

    wx = in_w_ref[0:1, :]
    wy = in_w_ref[1:2, :]
    wt = in_w_ref[2:3, :]
    wl = wx * wx + wy * wy
    for layer in (1, 2):
        w = hid_w_ref[layer]
        put_cat(w_cat, layer - 1, w)
        put_cat(wt_cat, layer - 1, w.T)
    w0 = hid_w_ref[0]
    for jet, scaled in enumerate((w0, w0 * wx, w0 * wy, w0 * wt, w0 * wl)):
        put_cat(w0_cat, jet, scaled)
        put_cat(wt0_cat, jet, scaled.T)
    out_high, out_low = split(out_w_ref[...])
    out_cat[...] = jnp.zeros_like(out_cat)
    out_cat[0:3, 0:256] = out_high
    out_cat[0:3, 256:512] = out_high
    out_cat[16:19, 0:256] = out_low
    rows = jnp.concatenate(
        [
            in_w_ref[...],
            in_b_ref[...],
            hid_b_ref[...],
            out_w_ref[...],
            jnp.zeros((6, WIDTH), F32),
        ],
        axis=0,
    )
    columns = rows.T
    for i in range(10):
        cols[i] = jnp.broadcast_to(columns[:, i : i + 1], (WIDTH, 128))
    grad_w[...] = jnp.zeros_like(grad_w)
    grad_g[...] = jnp.zeros_like(grad_g)
    partial[...] = jnp.zeros_like(partial)
    sums_buf[...] = jnp.zeros_like(sums_buf)

    def wide(i, r):
        c = cols[i, r, :]
        return jnp.concatenate([c, c], axis=1)

    chunks = [slice(c * ROWS, (c + 1) * ROWS) for c in range(CHUNKS)]

    def block(index, carry):
        base = pl.multiple_of(index * BLOCK, BLOCK)
        points = data_ref[:, pl.ds(base, BLOCK)]
        px = points[0:1, :]
        py = points[1:2, :]
        pt = points[2:3, :]
        slots = base + lax.broadcasted_iota(jnp.int32, (1, BLOCK), 1)
        mask = ((slots >= live_start) & (slots < live_start + live_count)).astype(F32)

        for r in chunks:
            z = wide(0, r) * px + wide(1, r) * py + wide(2, r) * pt + wide(3, r)
            h = jnp.tanh(z)
            s = 1.0 - h * h
            q = -2.0 * h * s
            h_buf[0, r, :] = h
            s_buf[0, r, :] = s
            for i, a in enumerate((h, s, q)):
                high, low = split(a)
                a0h_buf[i, r, :] = high
                a0l_buf[i, r, :] = low

        def forward_dot(layer, jet):
            if layer == 0:
                source = (0, 1, 1, 1, 2)[jet]
                high = a0h_buf[source]
                low = a0l_buf[source]
                w = w0_cat[jet]
            else:
                high = ah_buf[layer - 1, jet]
                low = al_buf[layer - 1, jet]
                w = w_cat[layer - 1]
            return matmul(w, jnp.concatenate([high, high, low], axis=0))

        for layer in range(3):
            top = layer == 2

            def put(jet, r, a):
                high, low = split(a)
                ah_buf[layer, jet, r, :] = high
                al_buf[layer, jet, r, :] = low
                if top:
                    a3_buf[jet, r, :] = a

            for jet in range(JETS):
                z_buf[layer, jet] = forward_dot(layer, jet)
            for r in chunks:
                h = jnp.tanh(z_buf[layer, 0, r, :] + wide(4 + layer, r))
                s = 1.0 - h * h
                q = -2.0 * h * s
                h_buf[layer + 1, r, :] = h
                s_buf[layer + 1, r, :] = s
                q_buf[layer, r, :] = q
                put(0, r, h)
            for jet in (1, 2, 3):
                for r in chunks:
                    put(jet, r, s_buf[layer + 1, r, :] * z_buf[layer, jet, r, :])
            for r in chunks:
                zx = z_buf[layer, 1, r, :]
                zy = z_buf[layer, 2, r, :]
                a = s_buf[layer + 1, r, :] * z_buf[layer, 4, r, :] + q_buf[layer, r, :] * (
                    zx * zx + zy * zy
                )
                put(4, r, a)

        outs = []
        for jet in range(JETS):
            both = matmul(
                out_cat[...],
                jnp.concatenate([ah_buf[2, jet], al_buf[2, jet]], axis=0),
            )
            outs.append(both[0:8] + both[16:24])
        u = outs[0][0:1] + out_b_ref[0]
        v = outs[0][1:2] + out_b_ref[1]
        u_x, v_x, p_x = outs[1][0:1], outs[1][1:2], outs[1][2:3]
        u_y, v_y, p_y = outs[2][0:1], outs[2][1:2], outs[2][2:3]
        u_t, v_t = outs[3][0:1], outs[3][1:2]
        u_l, v_l = outs[4][0:1], outs[4][1:2]
        cont = mask * (u_x + v_y)
        mom_x = mask * (u_t + u * u_x + v * u_y + p_x - VISCOSITY * u_l - points[3:4, :])
        mom_y = mask * (v_t + u * v_x + v * v_y + p_y - VISCOSITY * v_l - points[4:5, :])
        gc = 4.0 * cont
        gx = 2.0 * mom_x
        gy = 2.0 * mom_y
        du = gx * u_x + gy * v_x
        dv = gx * u_y + gy * v_y
        du_x = gc + gx * u
        dv_x = gy * u
        du_y = gx * v
        dv_y = gc + gy * v
        sums_buf[0:1, :] += cont * cont
        sums_buf[1:2, :] += mom_x * mom_x
        sums_buf[2:3, :] += mom_y * mom_y
        sums_buf[3:4, :] += du
        sums_buf[4:5, :] += dv

        def activation_back(a, r, g):
            h = h_buf[a, r, :]
            s = s_buf[a, r, :]
            zx = z_buf[a - 1, 1, r, :]
            zy = z_buf[a - 1, 2, r, :]
            zt = z_buf[a - 1, 3, r, :]
            zl = z_buf[a - 1, 4, r, :]
            g0, g1, g2, g3, g4 = g
            qg = 2.0 * (q_buf[a - 1, r, :] * g4)
            d_s = zx * g1 + zy * g2 + zt * g3 + zl * g4
            d_q = (zx * zx + zy * zy) * g4
            d0 = s * (g0 - 2.0 * (h * d_s) + (4.0 - 6.0 * s) * d_q)
            d1 = s * g1 + qg * zx
            d2 = s * g2 + qg * zy
            d3 = s * g3
            d4 = s * g4
            partial[a - 1, r, :] += fold(d0)
            for jet, d in enumerate((d0, d1, d2, d3, d4)):
                high, low = split(d)
                dzh_buf[a - 1, jet, r, :] = high
                dzl_buf[a - 1, jet, r, :] = low

        for r in chunks:
            wu = wide(7, r)
            wv = wide(8, r)
            wp = wide(9, r)
            g3 = wu * gx + wv * gy
            activation_back(
                3,
                r,
                (
                    wu * du + wv * dv,
                    wu * du_x + wv * dv_x + wp * gx,
                    wu * du_y + wv * dv_y + wp * gy,
                    g3,
                    -VISCOSITY * g3,
                ),
            )
            a0 = a3_buf[0, r, :]
            a1 = a3_buf[1, r, :]
            a2 = a3_buf[2, r, :]
            a34 = a3_buf[3, r, :] - VISCOSITY * a3_buf[4, r, :]
            partial[7, r, :] += fold(a0 * du + a1 * du_x + a2 * du_y + a34 * gx)
            partial[8, r, :] += fold(a0 * dv + a1 * dv_x + a2 * dv_y + a34 * gy)
            partial[9, r, :] += fold(a1 * gx + a2 * gy)

        for layer in (2, 1):
            for jet in range(JETS):
                high = dzh_buf[layer, jet]
                low = dzl_buf[layer, jet]
                g_buf[layer, jet] = matmul(
                    wt_cat[layer - 1], jnp.concatenate([high, high, low], axis=0)
                )
            left, right = [], []
            for jet in range(JETS):
                high = dzh_buf[layer, jet]
                left += [high, dzl_buf[layer, jet], high]
                a_high = ah_buf[layer - 1, jet]
                right += [a_high, a_high, al_buf[layer - 1, jet]]
            grad_w[layer - 1] += matmul_nt(
                jnp.concatenate(left, axis=1), jnp.concatenate(right, axis=1)
            )
            for r in chunks:
                activation_back(layer, r, [g_buf[layer, jet, r, :] for jet in range(JETS)])

        def stacked(jet):
            high = dzh_buf[0, jet]
            return [high, high, dzl_buf[0, jet]]

        g_buf[0, 0] = matmul(wt0_cat[0], jnp.concatenate(stacked(0), axis=0))
        g_buf[0, 1] = matmul(
            jnp.concatenate([wt0_cat[1], wt0_cat[2], wt0_cat[3]], axis=1),
            jnp.concatenate(stacked(1) + stacked(2) + stacked(3), axis=0),
        )
        g_buf[0, 2] = matmul(wt0_cat[4], jnp.concatenate(stacked(4), axis=0))
        for jet in range(JETS):
            source = (0, 1, 1, 1, 2)[jet]
            high = dzh_buf[0, jet]
            a_high = a0h_buf[source]
            grad_g[jet] += matmul_nt(
                jnp.concatenate([high, dzl_buf[0, jet], high], axis=1),
                jnp.concatenate([a_high, a_high, a0l_buf[source]], axis=1),
            )
        for r in chunks:
            h = h_buf[0, r, :]
            s = s_buf[0, r, :]
            d = s * (
                g_buf[0, 0, r, :]
                - 2.0 * (h * g_buf[0, 1, r, :])
                + (4.0 - 6.0 * s) * g_buf[0, 2, r, :]
            )
            partial[3, r, :] += fold(d * px)
            partial[4, r, :] += fold(d * py)
            partial[5, r, :] += fold(d * pt)
            partial[6, r, :] += fold(d)
        return carry

    lax.fori_loop(first_block, end_block, block, 0)

    def put_matrix(slot, value):
        packed_ref[slot * 512 : slot * 512 + 256, :] = value[:, :128]
        packed_ref[slot * 512 + 256 : slot * 512 + 512, :] = value[:, 128:]

    put_matrix(1, grad_w[0])
    put_matrix(2, grad_w[1])
    put_matrix(
        0,
        grad_g[0]
        + grad_g[1] * wx
        + grad_g[2] * wy
        + grad_g[3] * wt
        + grad_g[4] * wl,
    )
    by_l = 2.0 * jnp.sum(w0 * grad_g[4], axis=0, keepdims=True)
    direct = [
        jnp.sum(w0 * grad_g[1], axis=0, keepdims=True) + by_l * wx,
        jnp.sum(w0 * grad_g[2], axis=0, keepdims=True) + by_l * wy,
        jnp.sum(w0 * grad_g[3], axis=0, keepdims=True),
    ]
    lanes = lax.broadcasted_iota(jnp.int32, (WIDTH, 128), 1)
    placed = jnp.zeros((WIDTH, 128), F32)
    for i in range(10):
        placed = jnp.where(lanes == i, jnp.sum(partial[i], axis=1, keepdims=True), placed)
    small = placed.T[0:16]
    small_rows = [small[i : i + 1] for i in range(10)]
    for k in range(3):
        small_rows[3 + k] = small_rows[3 + k] + direct[k]
    totals = jnp.sum(sums_buf[...], axis=1, keepdims=True)
    lane = lax.broadcasted_iota(jnp.int32, (1, WIDTH), 1)
    scalars = jnp.where(lane == 6, live_count.astype(F32), 0.0)
    for at, row in ((0, 0), (1, 1), (2, 2), (3, 3), (4, 4)):
        scalars = jnp.where(lane == at, totals[row : row + 1], scalars)
    small_rows.append(scalars)
    block_small = jnp.concatenate(small_rows + [jnp.zeros((5, WIDTH), F32)], axis=0)
    packed_ref[SMALL_ROW : SMALL_ROW + 16, :] = block_small[:, :128]
    packed_ref[SMALL_ROW + 16 : SMALL_ROW + 32, :] = block_small[:, 128:]
    packed_ref[SMALL_ROW + 32 :, :] = jnp.zeros((PACKED_ROWS - SMALL_ROW - 32, 128), F32)


def local_terms(counts, offsets, data, in_w, in_b, hid_w, hid_b, out_w, out_b):
    vmem = pl.BlockSpec(memory_space=pltpu.VMEM)
    smem = pl.BlockSpec(memory_space=pltpu.SMEM)
    square = (WIDTH, BLOCK)
    return pl.pallas_call(
        step_kernel,
        out_shape=jax.ShapeDtypeStruct((PACKED_ROWS, 128), F32),
        in_specs=[smem, smem, vmem, vmem, vmem, vmem, vmem, vmem, smem],
        out_specs=vmem,
        scratch_shapes=[
            pltpu.VMEM((2, WIDTH, 768), BF16),
            pltpu.VMEM((2, WIDTH, 768), BF16),
            pltpu.VMEM((5, WIDTH, 768), BF16),
            pltpu.VMEM((5, WIDTH, 768), BF16),
            pltpu.VMEM((32, 512), BF16),
            pltpu.VMEM((10, WIDTH, 128), F32),
            pltpu.VMEM((3, JETS) + square, F32),
            pltpu.VMEM((4,) + square, F32),
            pltpu.VMEM((4,) + square, F32),
            pltpu.VMEM((3,) + square, F32),
            pltpu.VMEM((3, JETS) + square, BF16),
            pltpu.VMEM((3, JETS) + square, BF16),
            pltpu.VMEM((3,) + square, BF16),
            pltpu.VMEM((3,) + square, BF16),
            pltpu.VMEM((JETS,) + square, F32),
            pltpu.VMEM((3, JETS) + square, F32),
            pltpu.VMEM((3, JETS) + square, BF16),
            pltpu.VMEM((3, JETS) + square, BF16),
            pltpu.VMEM((2, WIDTH, WIDTH), F32),
            pltpu.VMEM((JETS, WIDTH, WIDTH), F32),
            pltpu.VMEM((10, WIDTH, 128), F32),
            pltpu.VMEM((8, BLOCK), F32),
        ],
        compiler_params=pltpu.CompilerParams(vmem_limit_bytes=60 * 1024 * 1024),
        name="pinn_step",
    )(counts, offsets, data, in_w, in_b.reshape(1, WIDTH), hid_w, hid_b, out_w, out_b)


def unpack_kernel(total_ref, in_w, in_b, hid_w, hid_b, out_w, out_b, means):
    scalars = total_ref[SMALL_ROW + 10 : SMALL_ROW + 11, :]
    scale = 1.0 / scalars[0:1, 6:7]
    for slot in range(3):
        hid_w[slot, :, 0:128] = total_ref[slot * 512 : slot * 512 + 256, :] * scale
        hid_w[slot, :, 128:256] = total_ref[slot * 512 + 256 : slot * 512 + 512, :] * scale

    def rows(first, count):
        at = SMALL_ROW + first
        left = total_ref[at : at + count, :]
        right = total_ref[at + 16 : at + 16 + count, :]
        return jnp.concatenate([left, right], axis=1) * scale

    hid_b[...] = rows(0, 3)
    in_w[...] = rows(3, 3)
    in_b[...] = rows(6, 1)
    out_w[...] = rows(7, 3)
    scaled = scalars * scale
    means[...] = scaled
    out_b[...] = scaled


def unpacked(total):
    vmem = pl.BlockSpec(memory_space=pltpu.VMEM)
    shapes = [(3, WIDTH), (1, WIDTH), (3, WIDTH, WIDTH), (3, WIDTH), (3, WIDTH), (1, 128), (1, 128)]
    in_w, in_b, hid_w, hid_b, out_w, out_b, means = pl.pallas_call(
        unpack_kernel,
        out_shape=[jax.ShapeDtypeStruct(s, F32) for s in shapes],
        in_specs=[vmem],
        out_specs=[vmem] * 7,
        name="unpack",
    )(total)
    return (
        in_w,
        in_b.reshape(WIDTH),
        hid_w,
        hid_b,
        out_w,
        out_b[0, 3:6],
        means[0, 0:3],
    )


def summed_over_devices(packed):
    half = PACKED_ROWS // 2
    core = lax.axis_index(NEAR)
    both = packed.reshape(2, half, 128)
    given = lax.dynamic_index_in_dim(both, 1 - core, 0, False)
    kept = lax.dynamic_index_in_dim(both, core, 0, False)
    mine = kept + lax.ppermute(given, NEAR, [(0, 1), (1, 0)])
    members = lax.axis_size(FAR)
    parts = lax.all_to_all(mine.reshape(members, half // members, 128), FAR, 0, 0, tiled=True)
    own = parts.sum(axis=0)
    spread = jnp.broadcast_to(own[None], (members,) + own.shape)
    gathered = lax.all_to_all(spread, FAR, 0, 0, tiled=True).reshape(half, 128)
    return lax.all_gather(gathered, NEAR, axis=0, tiled=True)


def shards(
    point_data,
    point_counts,
    point_offsets,
    in_weight,
    input_bias,
    hidden_layer_weight,
    hidden_bias,
    output_weight,
    out_bias,
):
    packed = local_terms(
        point_counts,
        point_offsets,
        point_data,
        in_weight,
        input_bias,
        hidden_layer_weight,
        hidden_bias,
        output_weight,
        out_bias,
    )
    return unpacked(summed_over_devices(packed))


def solution(mesh):
    torus = Mesh(mesh.devices.reshape(4, 4, 4, 2), PTS)
    placed = (P(None, PTS), P(PTS), P(PTS), P(), P(), P(), P(), P(), P())
    return jax.shard_map(
        shards,
        mesh=torus,
        in_specs=placed,
        out_specs=(P(), P(), P(), P(), P(), P(), P()),
        check_vma=False,
    )
```

time: 214 us -> 86.4 us (0.40)
  matrix products: 69.7 us -> 0 us
  blocking collectives: 86.9 us -> 45 us
  other arithmetic: 37.4 us -> 0.12 us
  Pallas kernels: 0 us -> 34.6 us
  local copies, waits for them, and re-layouts: 14.6 us -> 2.48 us
    dot_general x42 -> x0, matrix products: 69.7 us -> none  [the longest x27 51.7 us: network_jets(): jnp.einsum('hm,xmj->xhj', hidden_layer_weight[layer_apply], apply_tanh(st...]
    all_to_all x4 -> x2, blocking collectives: 86.9 us -> 39.7 us  [the longest x1 24.1 us: summed_over_devices(): lax.all_to_all(mine.reshape(members, half // members, 128), FAR, 0, 0, ti...]
    pallas_call x0 -> x2, Pallas kernels: none -> 34.6 us  [the longest x1 32.4 us: local_terms(): pl.pallas_call(step_kernel, out_shape=jax.ShapeDtypeStruct((PACKED_ROWS,...]
    mul x72 -> x0, other arithmetic: 17.6 us -> none  [the longest x3 4.33 us: residual_totals(): viscosity * (out[4, 0] + out[5, 0])]
    add x18 -> x1, other arithmetic: 6.99 us -> 0.05 us  [summed_over_devices(): mine = kept + lax.ppermute(given, NEAR, [(0, 1), (1, 0)])]
    all_gather x0 -> x1, blocking collectives: none -> 5.36 us  [summed_over_devices(): return lax.all_gather(gathered, NEAR, axis=0, tiled=True)]
    slice x7 -> x0, local copies, waits for them, and re-layouts: 5.23 us -> none  [the longest x3 2.4 us: network_jets(): stack_arrays = add_bias(stack_arrays, hidden_bias[layer_apply])]
    reduce_sum x23 -> x1, other arithmetic: 5.27 us -> 0.08 us  [summed_over_devices(): own = parts.sum(axis=0)]
  transfers between devices with their start and end apart: 0 -> 1, of which waited for: 0 -> 1; matrix products, arithmetic and copies ran while one was open for 0% -> 0% of each run, Pallas kernels for 0% -> 0%
where the time goes in v1:
time: 86.4 us; the launch traced here: 86.1 us
  blocking collectives  45 us (52%)
  Pallas kernels  34.6 us (40%)
  local copies, waits for them, and re-layouts  2.48 us (3%)
  between operations  1.97 us (2%)
  waiting for transfers between devices  1.76 us (2%)
    pallas_call x1, Pallas kernels, local_terms(): pl.pallas_call(step_kernel, out_shape=jax.ShapeDtypeStruct((PACKED_ROWS,...  32.4 us
    all_to_all x1, blocking collectives, summed_over_devices(): lax.all_to_all(mine.reshape(members, half // members, 128), FAR, 0, 0, ti...  24.1 us
    all_to_all x1, blocking collectives, summed_over_devices(): gathered = lax.all_to_all(spread, FAR, 0, 0, tiled=True).reshape(half, 128)  15.5 us
    all_gather x1, blocking collectives, summed_over_devices(): return lax.all_gather(gathered, NEAR, axis=0, tiled=True)  5.36 us
    pallas_call x1, Pallas kernels, unpacked(): pl.pallas_call(unpack_kernel, out_shape=[jax.ShapeDtypeStruct(s, F32) for...  2.2 us
    ppermute x1, waiting for transfers between devices, summed_over_devices(): mine = kept + lax.ppermute(given, NEAR, [(0, 1), (1, 0)])  1.76 us
  transfers between devices with their start and end apart: 1, of which 1 were waited for; matrix products, arithmetic and copies ran while one was open for 0% of the time, Pallas kernels for 0%

profile of v1, /device:TPU:1, one launch (start us, length us, event | category | flops | bytes accessed | tf_op | source)
XLA Modules:
  0.0 86.1 jit_solution(2279213176067246978)
XLA Ops:
  1.9 32.4 %pinn_step.1 = f32[1664,128]{1,0:T(8,128)} custom-call(s32[1]{0:T(128)S(6)} %copy.16.counts_ref, s32[1]{0:T(128)S(6)} %copy.17.offsets_ref, f32[5,1024]{1,0:T(8,128)} %data_ref.1, f32[3,256]{1,0:T(4,128)} %in_w_ref.1, f32[1,256]{1,0:T(1,128)} %bitcast.13, f32[3,256,256]{2,1,0:T(8,128)} %hid_w_ref.1, f32[3,256]{1,0:T(4,128)} %hid_b_ref.1, ...), custom_call_target="tpu_custom_call" | custom-call | tf_op jit(solution)/shard_map/pinn_step/pallas_call | solution.py:368
  34.4 0.0 copy-start
  34.4 1.1 %dynamic-slice_bitcast_fusion = f32[832,128]{1,0:T(8,128)S(1)} fusion(f32[2,832,128]{2,1,0:T(8,128)} %bitcast.11, s32[]{:T(128)S(6)} %select_n.8), kind=kLoop, calls=%fused_computation.1 | loop fusion | bytes 851972 | tf_op jit(solution)/shard_map/jit(dynamic_index_in_dim)/squeeze | solution.py:449
  35.5 0.1 collective-permute-start
  35.6 1.8 %collective-permute-done = f32[832,128]{1,0:T(8,128)S(1)} collective-permute-done((f32[832,128]{1,0:T(8,128)S(1)}, f32[832,128]{1,0:T(8,128)S(1)}, u32[]{:S(2)}, u32[]{:S(2)}) %collective-permute-start) | collective-permute-done | bytes 426016 | tf_op jit(solution)/shard_map/ppermute | solution.py:451
  37.3 0.0 copy-done
  37.4 24.1 %all_to_all.10 = f32[64,13,128]{2,1,0:T(8,128)S(1)} all-to-all(f32[64,13,128]{2,1,0:T(8,128)S(1)} %reshape.32), channel_id=1, replica_groups=mesh['pts_0'=4,'pts_1'=4,'pts_2'=4,'pts_3'=2] {'pts_0','pts_1','pts_2'}, dimensions={0} | all-to-all | bytes 851968 | tf_op jit(solution)/shard_map/all_to_all | solution.py:453
  61.6 0.1 reduce_sum.9
  61.7 15.5 %all_to_all.11 = f32[64,13,128]{2,1,0:T(8,128)S(1)} all-to-all(f32[64,13,128]{2,1,0:T(8,128)S(1)} %broadcast_in_dim.2), channel_id=1, replica_groups=mesh['pts_0'=4,'pts_1'=4,'pts_2'=4,'pts_3'=2] {'pts_0','pts_1','pts_2'}, dimensions={0} | all-to-all | bytes 851968 | tf_op jit(solution)/shard_map/all_to_all | solution.py:456
  77.3 5.4 %all_gather.3.total_ref = f32[1664,128]{1,0:T(8,128)} all-gather(f32[832,128]{1,0:T(8,128)S(1)} %reshape.33), channel_id=1, replica_groups=mesh['pts_0'=4,'pts_1'=4,'pts_2'=4,'pts_3'=2] {'pts_3'}, dimensions={0}, use_global_device_ids=true | all-gather | bytes 1277952 | tf_op jit(solution)/shard_map/all_gather | solution.py:457
  82.6 2.2 %unpack.1 = (f32[3,256]{1,0:T(4,128)}, f32[1,256]{1,0:T(1,128)}, f32[3,256,256]{2,1,0:T(8,128)}, f32[3,256]{1,0:T(4,128)}, f32[3,256]{1,0:T(4,128)}, /*index=5*/f32[1,128]{1,0:T(1,128)}, f32[1,128]{1,0:T(1,128)}) custom-call(f32[1664,128]{1,0:T(8,128)} %all_gather.3.total_ref), custom_call_target="tpu_custom_call" | custom-call | tf_op jit(solution)/shard_map/unpack/pallas_call | solution.py:427
  84.8 0.0 copy-start.1
  84.8 0.0 copy-start.2
  84.8 0.6 copy-done.1
  85.5 0.0 copy-done.2
  85.5 0.6 slice_bitcast_fusion
  (4 shorter events, 0.2 us)
Async XLA Ops:
  34.4 3.0 %copy-start = (f32[1664,128]{1,0:T(8,128)S(1)}, f32[1664,128]{1,0:T(8,128)}, u32[]{:S(2)}) copy-start(f32[1664,128]{1,0:T(8,128)} %pinn_step.1) | copy-start | bytes 2555908
  35.5 1.8 %collective-permute-start = (f32[832,128]{1,0:T(8,128)S(1)}, f32[832,128]{1,0:T(8,128)S(1)}, u32[]{:S(2)}, u32[]{:S(2)}) collective-permute-start(f32[832,128]{1,0:T(8,128)S(1)} %dynamic-slice_bitcast_fusion), channel_id=1, source_target_pairs={{0,1},{1,0},{2,3},{3,2},{4,5},{5,4},{6,7},{7,6},{8,9},{9,8},{10,11... | collective-permute-start | bytes 1277960 | tf_op jit(solution)/shard_map/ppermute | solution.py:451
  84.8 0.7 copy-start.1
  84.8 0.7 copy-start.2

commit v2 on v1

v2 whole, which is shorter than its diff:
```python
import functools

import jax
import jax.numpy as jnp
from jax import lax
from jax.experimental import pallas as pl
from jax.experimental.pallas import tpu as pltpu
from jax.sharding import Mesh
from jax.sharding import PartitionSpec as P

PTS = ("pts_0", "pts_1", "pts_2", "pts_3")
FAR = ("pts_0", "pts_1", "pts_2")
NEAR = "pts_3"

VISCOSITY = 0.2
HALF = 256
WIDTH = 256
ROWS = 16
F32 = jnp.float32
BF16 = jnp.bfloat16
JETS = 4
SMALL_ROW = 3 * 512
PACKED_ROWS = 1664
HALF_ROWS = PACKED_ROWS // 2
TILES = [
    (slice(r * ROWS, (r + 1) * ROWS), slice(c * 128, (c + 1) * 128))
    for r in range(WIDTH // ROWS)
    for c in range(HALF // 128)
]
PAIRS = 2


def split(x):
    high = x.astype(BF16)
    return high, (x - high.astype(F32)).astype(BF16)


def matmul(a, b):
    return lax.dot_general(a, b, (((1,), (0,)), ((), ())), preferred_element_type=F32)


def matmul_nt(a, b):
    return lax.dot_general(a, b, (((1,), (1,)), ((), ())), preferred_element_type=F32)


def step_kernel(
    core_ref,
    counts_ref,
    offsets_ref,
    data_ref,
    in_w_ref,
    in_b_ref,
    hid_w_ref,
    hid_b_ref,
    out_w_ref,
    out_b_ref,
    kept_ref,
    given_ref,
    w_cat,
    wt_cat,
    out_cat,
    outt_cat,
    cols,
    rows_buf,
    z_buf,
    h_buf,
    ah_buf,
    al_buf,
    a0h_buf,
    a0l_buf,
    g_buf,
    dzh_buf,
    dzl_buf,
    grads,
    partial,
    grad_out,
    sums_buf,
):
    live_start = offsets_ref[0]
    live_count = counts_ref[0]
    first_block = live_start // (2 * HALF * (PAIRS // 2))
    end_block = (live_start + live_count + 2 * HALF - 1) // (2 * HALF)

    def put_cat(ref, index, value):
        high, low = split(value)
        ref[index, :, 0:256] = high
        ref[index, :, 256:512] = low
        ref[index, :, 512:768] = high

    wx = in_w_ref[0:1, :]
    wy = in_w_ref[1:2, :]
    w0 = hid_w_ref[0]
    for index, w in enumerate((w0, w0 * wx, w0 * wy, hid_w_ref[1], hid_w_ref[2])):
        put_cat(w_cat, index, w)
        put_cat(wt_cat, index, w.T)
    out_high, out_low = split(out_w_ref[...])
    out_cat[...] = jnp.zeros_like(out_cat)
    out_cat[0:3, 0:256] = out_high
    out_cat[0:3, 256:512] = out_high
    out_cat[16:19, 0:256] = out_low
    spare = jnp.zeros((5, WIDTH), F32)
    out_rows = jnp.concatenate(
        [out_high.astype(F32), spare, out_low.astype(F32), spare, out_high.astype(F32), spare, jnp.zeros((8, WIDTH), F32)],
        axis=0,
    )
    outt_cat[...] = out_rows.T.astype(BF16)
    rows = jnp.concatenate(
        [
            in_w_ref[...],
            in_b_ref[...],
            hid_b_ref[...],
            wx * wx + wy * wy,
        ],
        axis=0,
    )
    columns = rows.T
    for i in range(8):
        cols[i] = jnp.broadcast_to(columns[:, i : i + 1], (WIDTH, 128))
    grads[...] = jnp.zeros_like(grads)
    partial[...] = jnp.zeros_like(partial)
    sums_buf[...] = jnp.zeros_like(sums_buf)
    grad_out[...] = jnp.zeros_like(grad_out)

    def chain(base, at):
        points = data_ref[:, pl.ds(base, HALF)]
        slots = base + lax.broadcasted_iota(jnp.int32, (1, HALF), 1)
        mask = ((slots >= live_start) & (slots < live_start + live_count)).astype(F32)

        def spread(i, row):
            rows_buf[at, i] = jnp.broadcast_to(row, (8, HALF))

        def row(i, lane):
            tile = rows_buf[at, i, :, lane]
            return jnp.concatenate([tile, tile], axis=0)

        for i in range(3):
            spread(i, points[i : i + 1, :])

        def put_split(high_ref, low_ref, where, value):
            high, low = split(value)
            high_ref[where] = high
            low_ref[where] = low

        for r, l in TILES:
            z = cols[0, r] * row(0, l) + cols[1, r] * row(1, l) + cols[2, r] * row(2, l) + cols[3, r]
            h = jnp.tanh(z)
            s = 1.0 - h * h
            h_buf[at, 0, r, l] = h
            d = s * cols[2, r] + (2.0 * VISCOSITY) * (h * s) * cols[7, r]
            for i, a in enumerate((h, s, d)):
                put_split(a0h_buf, a0l_buf, (at, i, r, l), a)
        yield

        def source(layer, jet):
            if layer == 0:
                i = (0, 1, 1, 2)[jet]
                return a0h_buf[at, i], a0l_buf[at, i]
            return ah_buf[at, layer - 1, jet], al_buf[at, layer - 1, jet]

        for layer in range(3):
            for jet in range(JETS):
                high, low = source(layer, jet)
                w = w_cat[(0, 1, 2, 0)[jet]] if layer == 0 else w_cat[layer + 2]
                z_buf[at, layer, jet] = matmul(w, jnp.concatenate([high, high, low], axis=0))
            yield
            for r, l in TILES:
                h = jnp.tanh(z_buf[at, layer, 0, r, l] + cols[4 + layer, r])
                s = 1.0 - h * h
                h_buf[at, layer + 1, r, l] = h
                zx = z_buf[at, layer, 1, r, l]
                zy = z_buf[at, layer, 2, r, l]
                d = s * z_buf[at, layer, 3, r, l] + (2.0 * VISCOSITY) * (h * s) * (
                    zx * zx + zy * zy
                )
                for jet, a in enumerate((h, s * zx, s * zy, d)):
                    put_split(ah_buf, al_buf, (at, layer, jet, r, l), a)
            yield

        outs = []
        for jet in range(JETS):
            high, low = source(3, jet)
            both = matmul(out_cat[...], jnp.concatenate([high, low], axis=0))
            outs.append(both[0:8] + both[16:24])
        u = outs[0][0:1] + out_b_ref[0]
        v = outs[0][1:2] + out_b_ref[1]
        u_x, v_x, p_x = outs[1][0:1], outs[1][1:2], outs[1][2:3]
        u_y, v_y, p_y = outs[2][0:1], outs[2][1:2], outs[2][2:3]
        u_d, v_d = outs[3][0:1], outs[3][1:2]
        cont = mask * (u_x + v_y)
        mom_x = mask * (u_d + u * u_x + v * u_y + p_x - points[3:4, :])
        mom_y = mask * (v_d + u * v_x + v * v_y + p_y - points[4:5, :])
        gc = 4.0 * cont
        gx = 2.0 * mom_x
        gy = 2.0 * mom_y
        du = gx * u_x + gy * v_x
        dv = gx * u_y + gy * v_y
        nothing = jnp.zeros_like(gx)
        cotangents = [
            jnp.concatenate([a, b, c] + [nothing] * 5, axis=0)
            for a, b, c in (
                (du, dv, nothing),
                (gc + gx * u, gy * u, gx),
                (gx * v, gc + gy * v, gy),
                (gx, gy, nothing),
            )
        ]
        sums_buf[0:1, :] += cont * cont
        sums_buf[1:2, :] += mom_x * mom_x
        sums_buf[2:3, :] += mom_y * mom_y
        sums_buf[3:4, :] += du
        sums_buf[4:5, :] += dv
        left, right = [], []
        for jet, value in enumerate(cotangents):
            high = value.astype(BF16).astype(F32)
            low = value - high
            g_buf[at, jet] = matmul(
                outt_cat[...],
                jnp.concatenate([high, high, low, jnp.zeros_like(low)], axis=0).astype(BF16),
            )
            pad = jnp.zeros_like(high)
            both = jnp.concatenate([high, pad, low, pad], axis=0).astype(BF16)
            alone = jnp.concatenate([high, pad, pad, pad], axis=0).astype(BF16)
            a_high, a_low = source(3, jet)
            left += [both, alone]
            right += [a_high, a_low]
        grad_out[...] += matmul_nt(jnp.concatenate(left, axis=1), jnp.concatenate(right, axis=1))
        yield

        def activation_back(a, r, l):
            h = h_buf[at, a, r, l]
            s = 1.0 - h * h
            zx = z_buf[at, a - 1, 1, r, l]
            zy = z_buf[at, a - 1, 2, r, l]
            zd = z_buf[at, a - 1, 3, r, l]
            square = zx * zx + zy * zy
            q = (2.0 * VISCOSITY) * (h * s)
            g0, g1, g2, g3 = [g_buf[at, jet, r, l] for jet in range(JETS)]
            qg = 2.0 * (q * g3)
            d_s = zx * g1 + zy * g2 + zd * g3
            d_q = square * g3
            d0 = s * (g0 - 2.0 * (h * d_s) + (6.0 * VISCOSITY * s - 4.0 * VISCOSITY) * d_q)
            d1 = s * g1 + qg * zx
            d2 = s * g2 + qg * zy
            partial[a - 1, r] += d0
            for jet, d in enumerate((d0, d1, d2, s * g3)):
                put_split(dzh_buf, dzl_buf, (at, a % 2, jet, r, l), d)

        for r, l in TILES:
            activation_back(3, r, l)
        yield

        for layer in (2, 1):
            up = (layer + 1) % 2
            for jet in range(JETS):
                high = dzh_buf[at, up, jet]
                g_buf[at, jet] = matmul(
                    wt_cat[layer + 2],
                    jnp.concatenate([high, high, dzl_buf[at, up, jet]], axis=0),
                )
            left, right = [], []
            for jet in range(JETS):
                high = dzh_buf[at, up, jet]
                left += [high, dzl_buf[at, up, jet], high]
                a_high, a_low = source(layer, jet)
                right += [a_high, a_high, a_low]
            grads[layer + 2] += matmul_nt(
                jnp.concatenate(left, axis=1), jnp.concatenate(right, axis=1)
            )
            yield
            for r, l in TILES:
                activation_back(layer, r, l)
            yield

        def stacked(jet):
            high = dzh_buf[at, 1, jet]
            return [high, high, dzl_buf[at, 1, jet]]

        g_buf[at, 0] = matmul(wt_cat[0], jnp.concatenate(stacked(0), axis=0))
        g_buf[at, 1] = matmul(
            jnp.concatenate([wt_cat[1], wt_cat[2]], axis=1),
            jnp.concatenate(stacked(1) + stacked(2), axis=0),
        )
        g_buf[at, 2] = matmul(wt_cat[0], jnp.concatenate(stacked(3), axis=0))
        for index, jets in enumerate(((0, 3), (1,), (2,))):
            left, right = [], []
            for jet in jets:
                high = dzh_buf[at, 1, jet]
                left += [high, dzl_buf[at, 1, jet], high]
                a_high, a_low = source(0, jet)
                right += [a_high, a_high, a_low]
            grads[index] += matmul_nt(
                jnp.concatenate(left, axis=1), jnp.concatenate(right, axis=1)
            )
        yield
        for r, l in TILES:
            h = h_buf[at, 0, r, l]
            s = 1.0 - h * h
            g3 = g_buf[at, 2, r, l]
            d_s = g_buf[at, 1, r, l] + cols[2, r] * g3
            d_q = cols[7, r] * g3
            d = s * (
                g_buf[at, 0, r, l]
                - 2.0 * (h * d_s)
                + (6.0 * VISCOSITY * s - 4.0 * VISCOSITY) * d_q
            )
            partial[3, r] += d * row(0, l)
            partial[4, r] += d * row(1, l)
            partial[5, r] += d * row(2, l) + s * g3
            partial[6, r] += d
            partial[7, r] += (2.0 * VISCOSITY) * (h * s) * g3
        yield

    def run(chains):
        queues = [[chains[i] for i in range(k, len(chains), 2)] for k in range(2)]
        started = False
        while any(queues):
            for k, queue in enumerate(queues):
                if k == 1 and not started:
                    started = True
                    continue
                while queue:
                    try:
                        next(queue[0])
                        break
                    except StopIteration:
                        queue.pop(0)

    if PAIRS == 4:
        run([chain(i * HALF, i % 2) for i in range(4)])
    else:

        def block(index, carry):
            base = pl.multiple_of(index * (2 * HALF), 2 * HALF)
            run([chain(pl.multiple_of(base + i * HALF, HALF), i) for i in range(2)])
            return carry

        lax.fori_loop(first_block, end_block, block, 0)

    wt = in_w_ref[2:3, :]
    grad0 = grads[0] + grads[1] * wx + grads[2] * wy
    direct = [
        jnp.sum(w0 * grads[1], axis=0, keepdims=True),
        jnp.sum(w0 * grads[2], axis=0, keepdims=True),
    ]
    lanes = lax.broadcasted_iota(jnp.int32, (WIDTH, 128), 1)
    placed = jnp.zeros((WIDTH, 128), F32)
    for i in range(8):
        placed = jnp.where(lanes == i, jnp.sum(partial[i], axis=1, keepdims=True), placed)
    small = placed.T[0:16]
    small_rows = [small[i : i + 1] for i in range(7)]
    small_rows.append(grad_out[0:3, :] + grad_out[16:19, :])
    by_square = 2.0 * small[7:8]
    small_rows[3] = small_rows[3] + direct[0] + by_square * wx
    small_rows[4] = small_rows[4] + direct[1] + by_square * wy
    totals = jnp.sum(sums_buf[...], axis=1, keepdims=True)
    lane = lax.broadcasted_iota(jnp.int32, (1, WIDTH), 1)
    scalars = jnp.where(lane == 6, live_count.astype(F32), 0.0)
    for at in range(5):
        scalars = jnp.where(lane == at, totals[at : at + 1], scalars)
    small_rows.append(scalars)
    block_small = jnp.concatenate(small_rows + [jnp.zeros((5, WIDTH), F32)], axis=0)
    pieces = [
        grad0[:, :128],
        grad0[:, 128:],
        grads[3, :, :128],
        grads[3, :, 128:],
        grads[4, :, :128],
        grads[4, :, 128:],
        block_small[:, :128],
        block_small[:, 128:],
        jnp.zeros((PACKED_ROWS - SMALL_ROW - 32, 128), F32),
    ]

    def pack(refs):
        begin = 0
        for piece in pieces:
            rows_left = piece.shape[0]
            done = 0
            while rows_left:
                which, inside = divmod(begin, HALF_ROWS)
                count = min(rows_left, HALF_ROWS - inside)
                refs[which][inside : inside + count, :] = piece[done : done + count]
                begin, done, rows_left = begin + count, done + count, rows_left - count

    @pl.when(core_ref[0] == 0)
    def _():
        pack((kept_ref, given_ref))

    @pl.when(core_ref[0] == 1)
    def _():
        pack((given_ref, kept_ref))


def local_terms(core, counts, offsets, data, in_w, in_b, hid_w, hid_b, out_w, out_b):
    vmem = pl.BlockSpec(memory_space=pltpu.VMEM)
    smem = pl.BlockSpec(memory_space=pltpu.SMEM)
    square = (WIDTH, HALF)
    half = jax.ShapeDtypeStruct((HALF_ROWS, 128), F32)
    return pl.pallas_call(
        step_kernel,
        out_shape=[half, half],
        in_specs=[smem, smem, smem, vmem, vmem, vmem, vmem, vmem, vmem, smem],
        out_specs=[vmem, vmem],
        scratch_shapes=[
            pltpu.VMEM((5, WIDTH, 768), BF16),
            pltpu.VMEM((5, WIDTH, 768), BF16),
            pltpu.VMEM((32, 512), BF16),
            pltpu.VMEM((WIDTH, 32), BF16),
            pltpu.VMEM((8, WIDTH, 128), F32),
            pltpu.VMEM((2, 3, 8, HALF), F32),
            pltpu.VMEM((2, 3, JETS) + square, F32),
            pltpu.VMEM((2, 4) + square, F32),
            pltpu.VMEM((2, 3, JETS) + square, BF16),
            pltpu.VMEM((2, 3, JETS) + square, BF16),
            pltpu.VMEM((2, 3) + square, BF16),
            pltpu.VMEM((2, 3) + square, BF16),
            pltpu.VMEM((2, JETS) + square, F32),
            pltpu.VMEM((2, 2, JETS) + square, BF16),
            pltpu.VMEM((2, 2, JETS) + square, BF16),
            pltpu.VMEM((5, WIDTH, WIDTH), F32),
            pltpu.VMEM((8, WIDTH, 128), F32),
            pltpu.VMEM((32, WIDTH), F32),
            pltpu.VMEM((8, HALF), F32),
        ],
        compiler_params=pltpu.CompilerParams(vmem_limit_bytes=44 * 1024 * 1024),
        name="pinn_step",
    )(core, counts, offsets, data, in_w, in_b.reshape(1, WIDTH), hid_w, hid_b, out_w, out_b)


def unpack_kernel(total_ref, in_w, in_b, hid_w, hid_b, out_w, out_b, means):
    scalars = total_ref[SMALL_ROW + 10 : SMALL_ROW + 11, :]
    scale = 1.0 / scalars[0:1, 6:7]
    for slot in range(3):
        hid_w[slot, :, 0:128] = total_ref[slot * 512 : slot * 512 + 256, :] * scale
        hid_w[slot, :, 128:256] = total_ref[slot * 512 + 256 : slot * 512 + 512, :] * scale

    def rows(first, count):
        at = SMALL_ROW + first
        left = total_ref[at : at + count, :]
        right = total_ref[at + 16 : at + 16 + count, :]
        return jnp.concatenate([left, right], axis=1) * scale

    hid_b[...] = rows(0, 3)
    in_w[...] = rows(3, 3)
    in_b[...] = rows(6, 1)
    out_w[...] = rows(7, 3)
    scaled = scalars * scale
    for i in range(3):
        means[i] = scaled[0, i]
        out_b[i] = scaled[0, 3 + i]


def unpacked(total):
    vmem = pl.BlockSpec(memory_space=pltpu.VMEM)
    shapes = [(3, WIDTH), (1, WIDTH), (3, WIDTH, WIDTH), (3, WIDTH), (3, WIDTH), (3,), (3,)]
    in_w, in_b, hid_w, hid_b, out_w, out_b, means = pl.pallas_call(
        unpack_kernel,
        out_shape=[jax.ShapeDtypeStruct(s, F32) for s in shapes],
        in_specs=[vmem],
        out_specs=[vmem] * 5 + [pl.BlockSpec(memory_space=pltpu.SMEM)] * 2,
        name="unpack",
    )(total)
    return (
        in_w,
        in_b.reshape(WIDTH),
        hid_w,
        hid_b,
        out_w,
        out_b,
        means,
    )


def summed_over_devices(kept, given):
    mine = kept + lax.ppermute(given, NEAR, [(0, 1), (1, 0)])
    members = lax.axis_size(FAR)
    parts = lax.all_to_all(mine.reshape(members, HALF_ROWS // members, 128), FAR, 0, 0, tiled=True)
    own = parts.sum(axis=0)
    spread = jnp.broadcast_to(own[None], (members,) + own.shape)
    gathered = lax.all_to_all(spread, FAR, 0, 0, tiled=True).reshape(HALF_ROWS, 128)
    return lax.all_gather(gathered, NEAR, axis=0, tiled=True)


def shards(
    point_data,
    point_counts,
    point_offsets,
    in_weight,
    input_bias,
    hidden_layer_weight,
    hidden_bias,
    output_weight,
    out_bias,
):
    kept, given = local_terms(
        lax.axis_index(NEAR).reshape(1),
        point_counts,
        point_offsets,
        point_data,
        in_weight,
        input_bias,
        hidden_layer_weight,
        hidden_bias,
        output_weight,
        out_bias,
    )
    return unpacked(summed_over_devices(kept, given))


def solution(mesh):
    torus = Mesh(mesh.devices.reshape(4, 4, 4, 2), PTS)
    placed = (P(None, PTS), P(PTS), P(PTS), P(), P(), P(), P(), P(), P())
    return jax.shard_map(
        shards,
        mesh=torus,
        in_specs=placed,
        out_specs=(P(), P(), P(), P(), P(), P(), P()),
        check_vma=False,
    )
```

time: 86.4 us -> 78.9 us (0.913)
  Pallas kernels: 34.6 us -> 26.2 us
  starting transfers between devices: 0.09 us -> 1.44 us
    pallas_call x1, Pallas kernels: 32.4 us -> 23.9 us  [local_terms(): pl.pallas_call(step_kernel, out_shape=[half, half], in_specs=[smem, smem,...]
    unnamed x6 -> x14, local copies, waits for them, and re-layouts: 0.67 us -> 3.2 us
    squeeze x2 -> x0, local copies, waits for them, and re-layouts: 1.69 us -> none  [the longest x1 1.11 us: summed_over_devices(): given = lax.dynamic_index_in_dim(both, 1 - core, 0, False)]
    ppermute x1, starting transfers between devices: 0.09 us -> 1.44 us  [summed_over_devices(): mine = kept + lax.ppermute(given, NEAR, [(0, 1), (1, 0)])]
where the time goes in v2:
time: 78.9 us; the launch traced here: 78.6 us
  blocking collectives  44.2 us (56%)
  Pallas kernels  26.2 us (33%)
  local copies, waits for them, and re-layouts  3.32 us (4%)
  between operations  2.04 us (3%)
  starting transfers between devices  1.44 us (2%)
  waiting for transfers between devices  1.4 us (2%)
    pallas_call x1, Pallas kernels, local_terms(): pl.pallas_call(step_kernel, out_shape=[half, half], in_specs=[smem, smem,...  23.9 us
    all_to_all x1, blocking collectives, summed_over_devices(): lax.all_to_all(mine.reshape(members, HALF_ROWS // members, 128), FAR, 0,...  23.3 us
    all_to_all x1, blocking collectives, summed_over_devices(): lax.all_to_all(spread, FAR, 0, 0, tiled=True).reshape(HALF_ROWS, 128)  15.5 us
    all_gather x1, blocking collectives, summed_over_devices(): return lax.all_gather(gathered, NEAR, axis=0, tiled=True)  5.36 us
    unnamed x14, local copies, waits for them, and re-layouts  3.2 us
    pallas_call x1, Pallas kernels, unpacked(): pl.pallas_call(unpack_kernel, out_shape=[jax.ShapeDtypeStruct(s, F32) for...  2.21 us
  transfers between devices with their start and end apart: 1, of which 1 were waited for; matrix products, arithmetic and copies ran while one was open for 0% of the time, Pallas kernels for 0%

profile of v2, /device:TPU:1, one launch (start us, length us, event | category | flops | bytes accessed | tf_op | source)
XLA Modules:
  0.0 78.6 jit_solution(17001519996741598074)
XLA Ops:
  0.6 0.0 copy-start.4
  0.6 0.0 copy-start.3
  0.7 0.0 copy-start.2
  2.0 0.0 copy-start.5
  2.0 0.0 copy-done.4
  2.0 0.0 copy-done.3
  2.0 0.0 copy-done.2
  2.0 0.6 copy-done.5
  2.7 0.0 copy-start
  2.7 1.1 %copy-done = f32[3,256,256]{2,1,0:T(8,128)S(1)} copy-done((f32[3,256,256]{2,1,0:T(8,128)S(1)}, f32[3,256,256]{2,1,0:T(8,128)}, u32[]{:S(2)}) %copy-start) | copy-done | bytes 786456
  3.8 0.0 copy-start.1
  3.8 0.8 copy-done.1
  4.6 0.0 copy-start.6
  4.6 0.7 copy-done.6
  5.2 23.9 %pinn_step.1 = (f32[832,128]{1,0:T(8,128)S(1)}, f32[832,128]{1,0:T(8,128)S(1)}) custom-call(s32[1]{0:T(128)} %bitcast.core_ref, s32[1]{0:T(128)S(6)} %copy.16.counts_ref, s32[1]{0:T(128)S(6)} %copy.17.offsets_ref, f32[5,1024]{1,0:T(8,128)S(1)} %copy-done.1, f32[3,256]{1,0:T(4,128)S(1)} %copy-done.2, f32[1,256]{1,0:T(1,128)S(1)} %bitcast.3, ...), custom_call_target="tpu_custom_call" | custom-call | tf_op jit(solution)/shard_map/pinn_step/pallas_call | solution.py:399
  29.2 1.4 %collective-permute-start = (f32[832,128]{1,0:T(8,128)S(1)}, f32[832,128]{1,0:T(8,128)S(1)}, u32[]{:S(2)}, u32[]{:S(2)}) collective-permute-start(f32[832,128]{1,0:T(8,128)S(1)} %get-tuple-element.17), channel_id=1, source_target_pairs={{0,1},{1,0},{2,3},{3,2},{4,5},{5,4},{6,7},{7,6},{8,9},{9,8},{10,11... | collective-permute-start | bytes 1277960 | tf_op jit(solution)/shard_map/ppermute | solution.py:475
  30.6 1.4 %collective-permute-done = f32[832,128]{1,0:T(8,128)S(1)} collective-permute-done((f32[832,128]{1,0:T(8,128)S(1)}, f32[832,128]{1,0:T(8,128)S(1)}, u32[]{:S(2)}, u32[]{:S(2)}) %collective-permute-start) | collective-permute-done | bytes 426016 | tf_op jit(solution)/shard_map/ppermute | solution.py:475
  32.1 23.3 %all_to_all.10 = f32[64,13,128]{2,1,0:T(8,128)S(1)} all-to-all(f32[64,13,128]{2,1,0:T(8,128)S(1)} %reshape.32), channel_id=1, replica_groups=mesh['pts_0'=4,'pts_1'=4,'pts_2'=4,'pts_3'=2] {'pts_0','pts_1','pts_2'}, dimensions={0} | all-to-all | bytes 851968 | tf_op jit(solution)/shard_map/all_to_all | solution.py:477
  55.4 0.1 reduce_sum.9
  55.5 15.5 %all_to_all.11 = f32[64,13,128]{2,1,0:T(8,128)S(1)} all-to-all(f32[64,13,128]{2,1,0:T(8,128)S(1)} %broadcast_in_dim.2), channel_id=1, replica_groups=mesh['pts_0'=4,'pts_1'=4,'pts_2'=4,'pts_3'=2] {'pts_0','pts_1','pts_2'}, dimensions={0} | all-to-all | bytes 851968 | tf_op jit(solution)/shard_map/all_to_all | solution.py:480
  71.1 5.4 %all_gather.3.total_ref = f32[1664,128]{1,0:T(8,128)} all-gather(f32[832,128]{1,0:T(8,128)S(1)} %reshape.33), channel_id=1, replica_groups=mesh['pts_0'=4,'pts_1'=4,'pts_2'=4,'pts_3'=2] {'pts_3'}, dimensions={0}, use_global_device_ids=true | all-gather | bytes 1277952 | tf_op jit(solution)/shard_map/all_gather | solution.py:481
  76.4 2.2 %unpack.1 = (f32[3,256]{1,0:T(4,128)}, f32[1,256]{1,0:T(1,128)}, f32[3,256,256]{2,1,0:T(8,128)}, f32[3,256]{1,0:T(4,128)}, f32[3,256]{1,0:T(4,128)}, /*index=5*/f32[3]{0:T(128)}, f32[3]{0:T(128)}) custom-call(f32[1664,128]{1,0:T(8,128)} %all_gather.3.total_ref), custom_call_target="tpu_custom_call" | custom-call | tf_op jit(solution)/shard_map/unpack/pallas_call | solution.py:456
  (4 shorter events, 0.2 us)
Async XLA Ops:
  0.6 1.4 %copy-start.4 = (f32[3,256]{1,0:T(4,128)S(1)}, f32[3,256]{1,0:T(4,128)}, u32[]{:S(2)}) copy-start(f32[3,256]{1,0:T(4,128)} %out_w_ref.1) | copy-start | bytes 9220
  0.6 1.4 %copy-start.3 = (f32[3,256]{1,0:T(4,128)S(1)}, f32[3,256]{1,0:T(4,128)}, u32[]{:S(2)}) copy-start(f32[3,256]{1,0:T(4,128)} %hid_b_ref.1) | copy-start | bytes 9220
  0.7 1.4 %copy-start.2 = (f32[3,256]{1,0:T(4,128)S(1)}, f32[3,256]{1,0:T(4,128)}, u32[]{:S(2)}) copy-start(f32[3,256]{1,0:T(4,128)} %in_w_ref.1) | copy-start | bytes 9220
  2.0 0.7 copy-start.5
  2.7 1.1 %copy-start = (f32[3,256,256]{2,1,0:T(8,128)S(1)}, f32[3,256,256]{2,1,0:T(8,128)}, u32[]{:S(2)}) copy-start(f32[3,256,256]{2,1,0:T(8,128)} %hid_w_ref.1) | copy-start | bytes 2359300
  3.8 0.8 copy-start.1
  4.6 0.7 copy-start.6
  29.2 2.8 %collective-permute-start = (f32[832,128]{1,0:T(8,128)S(1)}, f32[832,128]{1,0:T(8,128)S(1)}, u32[]{:S(2)}, u32[]{:S(2)}) collective-permute-start(f32[832,128]{1,0:T(8,128)S(1)} %get-tuple-element.17), channel_id=1, source_target_pairs={{0,1},{1,0},{2,3},{3,2},{4,5},{5,4},{6,7},{7,6},{8,9},{9,8},{10,11... | collective-permute-start | bytes 1277960 | tf_op jit(solution)/shard_map/ppermute | solution.py:475

commit v3 on v2

--- a/solution.py
+++ b/solution.py
@@ -47,6 +47,15 @@
     core_ref,
     counts_ref,
     offsets_ref,
+    data_hbm,
+    in_w_hbm,
+    in_b_hbm,
+    hid_w_hbm,
+    hid_b_hbm,
+    out_w_hbm,
+    out_b_hbm,
+    kept_ref,
+    given_ref,
     data_ref,
     in_w_ref,
     in_b_ref,
@@ -54,8 +63,7 @@
     hid_b_ref,
     out_w_ref,
     out_b_ref,
-    kept_ref,
-    given_ref,
+    copy_sems,
     w_cat,
     wt_cat,
     out_cat,
@@ -76,10 +84,34 @@
     grad_out,
     sums_buf,
 ):
+    copies = [
+        pltpu.make_async_copy(source, target, copy_sems.at[i])
+        for i, (source, target) in enumerate(
+            (
+                (in_w_hbm, in_w_ref),
+                (hid_w_hbm, hid_w_ref),
+                (in_b_hbm, in_b_ref),
+                (hid_b_hbm, hid_b_ref),
+                (out_w_hbm, out_w_ref),
+                (data_hbm, data_ref),
+                (out_b_hbm, out_b_ref),
+            )
+        )
+    ]
+    for copy in copies:
+        copy.start()
     live_start = offsets_ref[0]
     live_count = counts_ref[0]
     first_block = live_start // (2 * HALF * (PAIRS // 2))
     end_block = (live_start + live_count + 2 * HALF - 1) // (2 * HALF)
+
+    grads[...] = jnp.zeros_like(grads)
+    partial[...] = jnp.zeros_like(partial)
+    sums_buf[...] = jnp.zeros_like(sums_buf)
+    grad_out[...] = jnp.zeros_like(grad_out)
+    out_cat[...] = jnp.zeros_like(out_cat)
+    for copy in copies:
+        copy.wait()
 
     def put_cat(ref, index, value):
         high, low = split(value)
@@ -94,7 +126,6 @@
         put_cat(w_cat, index, w)
         put_cat(wt_cat, index, w.T)
     out_high, out_low = split(out_w_ref[...])
-    out_cat[...] = jnp.zeros_like(out_cat)
     out_cat[0:3, 0:256] = out_high
     out_cat[0:3, 256:512] = out_high
     out_cat[16:19, 0:256] = out_low
@@ -116,10 +147,6 @@
     columns = rows.T
     for i in range(8):
         cols[i] = jnp.broadcast_to(columns[:, i : i + 1], (WIDTH, 128))
-    grads[...] = jnp.zeros_like(grads)
-    partial[...] = jnp.zeros_like(partial)
-    sums_buf[...] = jnp.zeros_like(sums_buf)
-    grad_out[...] = jnp.zeros_like(grad_out)
 
     def chain(base, at):
         points = data_ref[:, pl.ds(base, HALF)]
@@ -396,12 +423,24 @@
     smem = pl.BlockSpec(memory_space=pltpu.SMEM)
     square = (WIDTH, HALF)
     half = jax.ShapeDtypeStruct((HALF_ROWS, 128), F32)
+    inputs = [
+        pltpu.with_memory_space_constraint(x, pltpu.HBM)
+        for x in (data, in_w, in_b.reshape(1, WIDTH), hid_w, hid_b, out_w, out_b)
+    ]
     return pl.pallas_call(
         step_kernel,
         out_shape=[half, half],
-        in_specs=[smem, smem, smem, vmem, vmem, vmem, vmem, vmem, vmem, smem],
+        in_specs=[smem] * 3 + [pl.BlockSpec(memory_space=pltpu.HBM)] * 7,
         out_specs=[vmem, vmem],
         scratch_shapes=[
+            pltpu.VMEM(data.shape, F32),
+            pltpu.VMEM((3, WIDTH), F32),
+            pltpu.VMEM((1, WIDTH), F32),
+            pltpu.VMEM((3, WIDTH, WIDTH), F32),
+            pltpu.VMEM((3, WIDTH), F32),
+            pltpu.VMEM((3, WIDTH), F32),
+            pltpu.SMEM((3,), F32),
+            pltpu.SemaphoreType.DMA((7,)),
             pltpu.VMEM((5, WIDTH, 768), BF16),
             pltpu.VMEM((5, WIDTH, 768), BF16),
             pltpu.VMEM((32, 512), BF16),
@@ -424,51 +463,70 @@
         ],
         compiler_params=pltpu.CompilerParams(vmem_limit_bytes=44 * 1024 * 1024),
         name="pinn_step",
-    )(core, counts, offsets, data, in_w, in_b.reshape(1, WIDTH), hid_w, hid_b, out_w, out_b)
-
-
-def unpack_kernel(total_ref, in_w, in_b, hid_w, hid_b, out_w, out_b, means):
-    scalars = total_ref[SMALL_ROW + 10 : SMALL_ROW + 11, :]
-    scale = 1.0 / scalars[0:1, 6:7]
-    for slot in range(3):
-        hid_w[slot, :, 0:128] = total_ref[slot * 512 : slot * 512 + 256, :] * scale
-        hid_w[slot, :, 128:256] = total_ref[slot * 512 + 256 : slot * 512 + 512, :] * scale
-
-    def rows(first, count):
-        at = SMALL_ROW + first
-        left = total_ref[at : at + count, :]
-        right = total_ref[at + 16 : at + 16 + count, :]
-        return jnp.concatenate([left, right], axis=1) * scale
-
-    hid_b[...] = rows(0, 3)
-    in_w[...] = rows(3, 3)
-    in_b[...] = rows(6, 1)
-    out_w[...] = rows(7, 3)
-    scaled = scalars * scale
-    for i in range(3):
-        means[i] = scaled[0, i]
-        out_b[i] = scaled[0, 3 + i]
-
-
-def unpacked(total):
+    )(core, counts, offsets, *inputs)
+
+
+def unpack_kernel(
+    core_ref, own_ref, other_ref, in_w, in_b, hid_w_hbm, hid_b, out_w, out_b, means, hid_w, copy_sems
+):
+    def fill(halves):
+        def rows(begin, count):
+            parts = []
+            while count:
+                which, inside = divmod(begin, HALF_ROWS)
+                taken = min(count, HALF_ROWS - inside)
+                parts.append(halves[which][inside : inside + taken, :])
+                begin, count = begin + taken, count - taken
+            return parts[0] if len(parts) == 1 else jnp.concatenate(parts, axis=0)
+
+        small = jnp.concatenate([rows(SMALL_ROW, 16), rows(SMALL_ROW + 16, 16)], axis=1)
+        scalars = small[10:11]
+        scale = 1.0 / scalars[0:1, 6:7]
+        copies = []
+        for slot in range(3):
+            hid_w[slot, :, 0:128] = rows(slot * 512, 256) * scale
+            hid_w[slot, :, 128:256] = rows(slot * 512 + 256, 256) * scale
+            copies.append(
+                pltpu.make_async_copy(hid_w.at[slot], hid_w_hbm.at[slot], copy_sems.at[slot])
+            )
+            copies[-1].start()
+        scaled = small * scale
+        hid_b[...] = scaled[0:3]
+        in_w[...] = scaled[3:6]
+        in_b[...] = scaled[6:7]
+        out_w[...] = scaled[7:10]
+        for i in range(3):
+            means[i] = scaled[10, i]
+            out_b[i] = scaled[10, 3 + i]
+        for copy in copies:
+            copy.wait()
+
+    @pl.when(core_ref[0] == 0)
+    def _():
+        fill((own_ref, other_ref))
+
+    @pl.when(core_ref[0] == 1)
+    def _():
+        fill((other_ref, own_ref))
+
+
+def unpacked(core, own, other):
     vmem = pl.BlockSpec(memory_space=pltpu.VMEM)
+    smem = pl.BlockSpec(memory_space=pltpu.SMEM)
     shapes = [(3, WIDTH), (1, WIDTH), (3, WIDTH, WIDTH), (3, WIDTH), (3, WIDTH), (3,), (3,)]
     in_w, in_b, hid_w, hid_b, out_w, out_b, means = pl.pallas_call(
         unpack_kernel,
         out_shape=[jax.ShapeDtypeStruct(s, F32) for s in shapes],
-        in_specs=[vmem],
-        out_specs=[vmem] * 5 + [pl.BlockSpec(memory_space=pltpu.SMEM)] * 2,
+        in_specs=[smem, vmem, vmem],
+        out_specs=[vmem, vmem, pl.BlockSpec(memory_space=pltpu.HBM), vmem, vmem, smem, smem],
+        scratch_shapes=[
+            pltpu.VMEM((3, WIDTH, WIDTH), F32),
+            pltpu.SemaphoreType.DMA((3,)),
+        ],
+        compiler_params=pltpu.CompilerParams(vmem_limit_bytes=8 * 1024 * 1024),
         name="unpack",
-    )(total)
-    return (
-        in_w,
-        in_b.reshape(WIDTH),
-        hid_w,
-        hid_b,
-        out_w,
-        out_b,
-        means,
-    )
+    )(core, own, other)
+    return in_w, in_b.reshape(WIDTH), hid_w, hid_b, out_w, out_b, means
 
 
 def summed_over_devices(kept, given):
@@ -477,8 +535,8 @@
     parts = lax.all_to_all(mine.reshape(members, HALF_ROWS // members, 128), FAR, 0, 0, tiled=True)
     own = parts.sum(axis=0)
     spread = jnp.broadcast_to(own[None], (members,) + own.shape)
-    gathered = lax.all_to_all(spread, FAR, 0, 0, tiled=True).reshape(HALF_ROWS, 128)
-    return lax.all_gather(gathered, NEAR, axis=0, tiled=True)
+    own = lax.all_to_all(spread, FAR, 0, 0, tiled=True).reshape(HALF_ROWS, 128)
+    return own, lax.ppermute(own, NEAR, [(0, 1), (1, 0)])
 
 
 def shards(
@@ -492,8 +550,9 @@
     output_weight,
     out_bias,
 ):
+    core = lax.axis_index(NEAR).reshape(1)
     kept, given = local_terms(
-        lax.axis_index(NEAR).reshape(1),
+        core,
         point_counts,
         point_offsets,
         point_data,
@@ -504,7 +563,7 @@
         output_weight,
         out_bias,
     )
-    return unpacked(summed_over_devices(kept, given))
+    return unpacked(core, *summed_over_devices(kept, given))
 
 
 def solution(mesh):

time: 78.9 us -> 74.9 us (0.949)
  blocking collectives: 44.2 us -> 38.8 us
  starting transfers between devices: 1.44 us -> 4.71 us
  local copies, waits for them, and re-layouts: 3.32 us -> 0.12 us
  waiting for transfers between devices: 1.4 us -> 2.79 us
    all_gather x1 -> x0, blocking collectives: 5.36 us -> none  [summed_over_devices(): return lax.all_gather(gathered, NEAR, axis=0, tiled=True)]
    ppermute x0 -> x1, starting transfers between devices: none -> 3.27 us  [summed_over_devices(): return (own, lax.ppermute(own, NEAR, [(0, 1), (1, 0)]))]
    unnamed x14 -> x0, local copies, waits for them, and re-layouts: 3.2 us -> none
    ppermute x0 -> x1, waiting for transfers between devices: none -> 1.4 us  [summed_over_devices(): return (own, lax.ppermute(own, NEAR, [(0, 1), (1, 0)]))]
  transfers between devices with their start and end apart: 1 -> 2, of which waited for: 1 -> 2; matrix products, arithmetic and copies ran while one was open for 0% -> 0% of each run, Pallas kernels for 0% -> 0%
where the time goes in v3:
time: 74.9 us; the launch traced here: 74.7 us
  blocking collectives  38.8 us (52%)
  Pallas kernels  26.2 us (35%)
  starting transfers between devices  4.71 us (6%)
  waiting for transfers between devices  2.79 us (4%)
  between operations  1.96 us (3%)
    pallas_call x1, Pallas kernels, local_terms(): pl.pallas_call(step_kernel, out_shape=[half, half], in_specs=[smem] * 3 +...  24.5 us
    all_to_all x1, blocking collectives, summed_over_devices(): lax.all_to_all(mine.reshape(members, HALF_ROWS // members, 128), FAR, 0,...  23.3 us
    all_to_all x1, blocking collectives, summed_over_devices(): own = lax.all_to_all(spread, FAR, 0, 0, tiled=True).reshape(HALF_ROWS, 128)  15.5 us
    ppermute x1, starting transfers between devices, summed_over_devices(): return (own, lax.ppermute(own, NEAR, [(0, 1), (1, 0)]))  3.27 us
    pallas_call x1, Pallas kernels, unpacked(): pl.pallas_call(unpack_kernel, out_shape=[jax.ShapeDtypeStruct(s, F32) for...  1.64 us
  transfers between devices with their start and end apart: 2, of which 2 were waited for; matrix products, arithmetic and copies ran while one was open for 0% of the time, Pallas kernels for 0%

profile of v3, /device:TPU:1, one launch (start us, length us, event | category | flops | bytes accessed | tf_op | source)
XLA Modules:
  0.0 74.7 jit_solution(128703384437592156)
XLA Ops:
  1.9 24.5 %pinn_step.1 = (f32[832,128]{1,0:T(8,128)S(1)}, f32[832,128]{1,0:T(8,128)S(1)}) custom-call(s32[1]{0:T(128)} %bitcast.core_ref, s32[1]{0:T(128)S(6)} %copy.16.counts_ref, s32[1]{0:T(128)S(6)} %copy.17.offsets_ref, f32[5,1024]{1,0:T(8,128)} %data_hbm.1, f32[3,256]{1,0:T(4,128)} %in_w_hbm.1, f32[1,256]{1,0:T(1,128)} %bitcast.3, f32[3,256,256]{2,1,0:T(8,128)} %hid_w_hbm.1, ...), custom_call_target="tpu_custom_call" | custom-call | tf_op jit(solution)/shard_map/pinn_step/pallas_call | solution.py:430
  26.5 1.4 %collective-permute-start = (f32[832,128]{1,0:T(8,128)S(1)}, f32[832,128]{1,0:T(8,128)S(1)}, u32[]{:S(2)}, u32[]{:S(2)}) collective-permute-start(f32[832,128]{1,0:T(8,128)S(1)} %get-tuple-element.17), channel_id=1, source_target_pairs={{0,1},{1,0},{2,3},{3,2},{4,5},{5,4},{6,7},{7,6},{8,9},{9,8},{10,11... | collective-permute-start | bytes 1277960 | tf_op jit(solution)/shard_map/ppermute | solution.py:533
  27.9 1.4 %collective-permute-done = f32[832,128]{1,0:T(8,128)S(1)} collective-permute-done((f32[832,128]{1,0:T(8,128)S(1)}, f32[832,128]{1,0:T(8,128)S(1)}, u32[]{:S(2)}, u32[]{:S(2)}) %collective-permute-start) | collective-permute-done | bytes 426016 | tf_op jit(solution)/shard_map/ppermute | solution.py:533
  29.4 23.3 %all_to_all.10 = f32[64,13,128]{2,1,0:T(8,128)S(1)} all-to-all(f32[64,13,128]{2,1,0:T(8,128)S(1)} %reshape.32), channel_id=1, replica_groups=mesh['pts_0'=4,'pts_1'=4,'pts_2'=4,'pts_3'=2] {'pts_0','pts_1','pts_2'}, dimensions={0} | all-to-all | bytes 851968 | tf_op jit(solution)/shard_map/all_to_all | solution.py:535
  52.7 0.1 reduce_sum.9
  52.8 15.5 %all_to_all.11 = f32[64,13,128]{2,1,0:T(8,128)S(1)} all-to-all(f32[64,13,128]{2,1,0:T(8,128)S(1)} %broadcast_in_dim.2), channel_id=1, replica_groups=mesh['pts_0'=4,'pts_1'=4,'pts_2'=4,'pts_3'=2] {'pts_0','pts_1','pts_2'}, dimensions={0} | all-to-all | bytes 851968 | tf_op jit(solution)/shard_map/all_to_all | solution.py:538
  68.4 3.3 %collective-permute-start.1 = (f32[832,128]{1,0:T(8,128)S(1)}, f32[832,128]{1,0:T(8,128)S(1)}, u32[]{:S(2)}, u32[]{:S(2)}) collective-permute-start(f32[832,128]{1,0:T(8,128)S(1)} %reshape.33.own_ref), channel_id=1, source_target_pairs={{0,1},{1,0},{2,3},{3,2},{4,5},{5,4},{6,7},{7,6},{8,9},{9,8},{10,11... | collective-permute-start | bytes 1277960 | tf_op jit(solution)/shard_map/ppermute | solution.py:539
  71.7 1.4 %collective-permute-done.1.other_ref = f32[832,128]{1,0:T(8,128)S(1)} collective-permute-done((f32[832,128]{1,0:T(8,128)S(1)}, f32[832,128]{1,0:T(8,128)S(1)}, u32[]{:S(2)}, u32[]{:S(2)}) %collective-permute-start.1) | collective-permute-done | bytes 426016 | tf_op jit(solution)/shard_map/ppermute | solution.py:539
  73.1 1.6 %unpack.1 = (f32[3,256]{1,0:T(4,128)}, f32[1,256]{1,0:T(1,128)}, f32[3,256,256]{2,1,0:T(8,128)}, f32[3,256]{1,0:T(4,128)}, f32[3,256]{1,0:T(4,128)}, /*index=5*/f32[3]{0:T(128)}, f32[3]{0:T(128)}) custom-call(s32[1]{0:T(128)} %bitcast.core_ref, f32[832,128]{1,0:T(8,128)S(1)} %reshape.33.own_ref, f32[832,128]{1,0:T(8,128)S(1)} %collective-permute-done.1.other_ref), custom_call_target="tpu_custom_call" | custom-call | tf_op jit(solution)/shard_map/unpack/pallas_call | solution.py:517
  (4 shorter events, 0.2 us)
Async XLA Ops:
  26.5 2.8 %collective-permute-start = (f32[832,128]{1,0:T(8,128)S(1)}, f32[832,128]{1,0:T(8,128)S(1)}, u32[]{:S(2)}, u32[]{:S(2)}) collective-permute-start(f32[832,128]{1,0:T(8,128)S(1)} %get-tuple-element.17), channel_id=1, source_target_pairs={{0,1},{1,0},{2,3},{3,2},{4,5},{5,4},{6,7},{7,6},{8,9},{9,8},{10,11... | collective-permute-start | bytes 1277960 | tf_op jit(solution)/shard_map/ppermute | solution.py:533
  68.4 4.7 %collective-permute-start.1 = (f32[832,128]{1,0:T(8,128)S(1)}, f32[832,128]{1,0:T(8,128)S(1)}, u32[]{:S(2)}, u32[]{:S(2)}) collective-permute-start(f32[832,128]{1,0:T(8,128)S(1)} %reshape.33.own_ref), channel_id=1, source_target_pairs={{0,1},{1,0},{2,3},{3,2},{4,5},{5,4},{6,7},{7,6},{8,9},{9,8},{10,11... | collective-permute-start | bytes 1277960 | tf_op jit(solution)/shard_map/ppermute | solution.py:539

commit v4 on v3

--- a/solution.py
+++ b/solution.py
@@ -19,15 +19,19 @@
 F32 = jnp.float32
 BF16 = jnp.bfloat16
 JETS = 4
-SMALL_ROW = 3 * 512
-PACKED_ROWS = 1664
-HALF_ROWS = PACKED_ROWS // 2
+HALF_ROWS = 832
+PIECES = (
+    ((0, 0, 0, 256, 0), (0, 1, 0, 256, 256), (1, 0, 0, 256, 512), (1, 1, 0, 48, 768)),
+    ((1, 1, 48, 208, 0), (2, 0, 0, 256, 208), (2, 1, 0, 256, 464)),
+)
+SMALL_ROW = 720
+COUNT_ROWS = (816, 752)
 TILES = [
     (slice(r * ROWS, (r + 1) * ROWS), slice(c * 128, (c + 1) * 128))
     for r in range(WIDTH // ROWS)
     for c in range(HALF // 128)
 ]
-PAIRS = 2
+OFFSET = 3
 
 
 def split(x):
@@ -44,7 +48,6 @@
 
 
 def step_kernel(
-    core_ref,
     counts_ref,
     offsets_ref,
     data_hbm,
@@ -89,10 +92,10 @@
         for i, (source, target) in enumerate(
             (
                 (in_w_hbm, in_w_ref),
-                (hid_w_hbm, hid_w_ref),
                 (in_b_hbm, in_b_ref),
                 (hid_b_hbm, hid_b_ref),
                 (out_w_hbm, out_w_ref),
+                (hid_w_hbm, hid_w_ref),
                 (data_hbm, data_ref),
                 (out_b_hbm, out_b_ref),
             )
@@ -100,18 +103,36 @@
     ]
     for copy in copies:
         copy.start()
-    live_start = offsets_ref[0]
-    live_count = counts_ref[0]
-    first_block = live_start // (2 * HALF * (PAIRS // 2))
-    end_block = (live_start + live_count + 2 * HALF - 1) // (2 * HALF)
-
+    core = lax.axis_index(NEAR)
     grads[...] = jnp.zeros_like(grads)
     partial[...] = jnp.zeros_like(partial)
     sums_buf[...] = jnp.zeros_like(sums_buf)
     grad_out[...] = jnp.zeros_like(grad_out)
     out_cat[...] = jnp.zeros_like(out_cat)
-    for copy in copies:
+    for copy in copies[:4]:
         copy.wait()
+
+    wx = in_w_ref[0:1, :]
+    wy = in_w_ref[1:2, :]
+    rows = jnp.concatenate(
+        [
+            in_w_ref[...],
+            in_b_ref[...],
+            hid_b_ref[...],
+            wx * wx + wy * wy,
+        ],
+        axis=0,
+    )
+    columns = rows.T
+    for i in range(8):
+        cols[i] = jnp.broadcast_to(columns[:, i : i + 1], (WIDTH, 128))
+
+    for copy in copies[4:]:
+        copy.wait()
+    live_start = offsets_ref[0]
+    live_count = counts_ref[0]
+    first_block = live_start // (2 * HALF)
+    end_block = (live_start + live_count + 2 * HALF - 1) // (2 * HALF)
 
     def put_cat(ref, index, value):
         high, low = split(value)
@@ -119,8 +140,6 @@
         ref[index, :, 256:512] = low
         ref[index, :, 512:768] = high
 
-    wx = in_w_ref[0:1, :]
-    wy = in_w_ref[1:2, :]
     w0 = hid_w_ref[0]
     for index, w in enumerate((w0, w0 * wx, w0 * wy, hid_w_ref[1], hid_w_ref[2])):
         put_cat(w_cat, index, w)
@@ -135,19 +154,6 @@
         axis=0,
     )
     outt_cat[...] = out_rows.T.astype(BF16)
-    rows = jnp.concatenate(
-        [
-            in_w_ref[...],
-            in_b_ref[...],
-            hid_b_ref[...],
-            wx * wx + wy * wy,
-        ],
-        axis=0,
-    )
-    columns = rows.T
-    for i in range(8):
-        cols[i] = jnp.broadcast_to(columns[:, i : i + 1], (WIDTH, 128))
-
     def chain(base, at):
         points = data_ref[:, pl.ds(base, HALF)]
         slots = base + lax.broadcasted_iota(jnp.int32, (1, HALF), 1)
@@ -260,14 +266,13 @@
             zy = z_buf[at, a - 1, 2, r, l]
             zd = z_buf[at, a - 1, 3, r, l]
             square = zx * zx + zy * zy
-            q = (2.0 * VISCOSITY) * (h * s)
             g0, g1, g2, g3 = [g_buf[at, jet, r, l] for jet in range(JETS)]
-            qg = 2.0 * (q * g3)
+            k = ((4.0 * VISCOSITY) * h) * g3
             d_s = zx * g1 + zy * g2 + zd * g3
             d_q = square * g3
             d0 = s * (g0 - 2.0 * (h * d_s) + (6.0 * VISCOSITY * s - 4.0 * VISCOSITY) * d_q)
-            d1 = s * g1 + qg * zx
-            d2 = s * g2 + qg * zy
+            d1 = s * (g1 + k * zx)
+            d2 = s * (g2 + k * zy)
             partial[a - 1, r] += d0
             for jet, d in enumerate((d0, d1, d2, s * g3)):
                 put_split(dzh_buf, dzl_buf, (at, a % 2, jet, r, l), d)
@@ -338,30 +343,21 @@
         yield
 
     def run(chains):
-        queues = [[chains[i] for i in range(k, len(chains), 2)] for k in range(2)]
-        started = False
-        while any(queues):
-            for k, queue in enumerate(queues):
-                if k == 1 and not started:
-                    started = True
-                    continue
-                while queue:
-                    try:
-                        next(queue[0])
-                        break
-                    except StopIteration:
-                        queue.pop(0)
-
-    if PAIRS == 4:
-        run([chain(i * HALF, i % 2) for i in range(4)])
-    else:
-
-        def block(index, carry):
-            base = pl.multiple_of(index * (2 * HALF), 2 * HALF)
-            run([chain(pl.multiple_of(base + i * HALF, HALF), i) for i in range(2)])
-            return carry
-
-        lax.fori_loop(first_block, end_block, block, 0)
+        waiting = list(chains)
+        at = 0
+        while waiting:
+            for k, stages in enumerate(chains):
+                if stages in waiting and (k == 0 or at >= OFFSET):
+                    if next(stages, "end") == "end":
+                        waiting.remove(stages)
+            at += 1
+
+    def block(index, carry):
+        base = pl.multiple_of(index * (2 * HALF), 2 * HALF)
+        run([chain(pl.multiple_of(base + i * HALF, HALF), i) for i in range(2)])
+        return carry
+
+    lax.fori_loop(first_block, end_block, block, 0)
 
     wt = in_w_ref[2:3, :]
     grad0 = grads[0] + grads[1] * wx + grads[2] * wy
@@ -381,46 +377,38 @@
     small_rows[4] = small_rows[4] + direct[1] + by_square * wy
     totals = jnp.sum(sums_buf[...], axis=1, keepdims=True)
     lane = lax.broadcasted_iota(jnp.int32, (1, WIDTH), 1)
-    scalars = jnp.where(lane == 6, live_count.astype(F32), 0.0)
+    scalars = jnp.zeros((1, WIDTH), F32)
     for at in range(5):
         scalars = jnp.where(lane == at, totals[at : at + 1], scalars)
     small_rows.append(scalars)
     block_small = jnp.concatenate(small_rows + [jnp.zeros((5, WIDTH), F32)], axis=0)
-    pieces = [
-        grad0[:, :128],
-        grad0[:, 128:],
-        grads[3, :, :128],
-        grads[3, :, 128:],
-        grads[4, :, :128],
-        grads[4, :, 128:],
-        block_small[:, :128],
-        block_small[:, 128:],
-        jnp.zeros((PACKED_ROWS - SMALL_ROW - 32, 128), F32),
-    ]
+    count_rows = jnp.broadcast_to(live_count.astype(F32), (8, 128))
 
     def pack(refs):
-        begin = 0
-        for piece in pieces:
-            rows_left = piece.shape[0]
-            done = 0
-            while rows_left:
-                which, inside = divmod(begin, HALF_ROWS)
-                count = min(rows_left, HALF_ROWS - inside)
-                refs[which][inside : inside + count, :] = piece[done : done + count]
-                begin, done, rows_left = begin + count, done + count, rows_left - count
-
-    @pl.when(core_ref[0] == 0)
+        for ref, pieces, count_row in zip(refs, PIECES, COUNT_ROWS):
+            for layer, side, first, rows, at in pieces:
+                columns = slice(side * 128, side * 128 + 128)
+                if layer == 0:
+                    value = grad0[first : first + rows, columns]
+                else:
+                    value = grads[layer + 2, first : first + rows, columns]
+                ref[at : at + rows, :] = value
+            ref[count_row : count_row + 8, :] = count_rows
+            ref[count_row + 8 :, :] = jnp.zeros((HALF_ROWS - count_row - 8, 128), F32)
+        refs[1][SMALL_ROW : SMALL_ROW + 16, :] = block_small[:, :128]
+        refs[1][SMALL_ROW + 16 : SMALL_ROW + 32, :] = block_small[:, 128:]
+
+    @pl.when(core == 0)
     def _():
         pack((kept_ref, given_ref))
 
-    @pl.when(core_ref[0] == 1)
+    @pl.when(core == 1)
     def _():
         pack((given_ref, kept_ref))
 
 
-def local_terms(core, counts, offsets, data, in_w, in_b, hid_w, hid_b, out_w, out_b):
+def local_terms(counts, offsets, data, in_w, in_b, hid_w, hid_b, out_w, out_b):
     vmem = pl.BlockSpec(memory_space=pltpu.VMEM)
-    smem = pl.BlockSpec(memory_space=pltpu.SMEM)
     square = (WIDTH, HALF)
     half = jax.ShapeDtypeStruct((HALF_ROWS, 128), F32)
     inputs = [
@@ -430,7 +418,8 @@
     return pl.pallas_call(
         step_kernel,
         out_shape=[half, half],
-        in_specs=[smem] * 3 + [pl.BlockSpec(memory_space=pltpu.HBM)] * 7,
+        in_specs=[pl.BlockSpec(memory_space=pltpu.SMEM)] * 2
+        + [pl.BlockSpec(memory_space=pltpu.HBM)] * 7,
         out_specs=[vmem, vmem],
         scratch_shapes=[
             pltpu.VMEM(data.shape, F32),
@@ -463,69 +452,91 @@
         ],
         compiler_params=pltpu.CompilerParams(vmem_limit_bytes=44 * 1024 * 1024),
         name="pinn_step",
-    )(core, counts, offsets, *inputs)
-
-
-def unpack_kernel(
-    core_ref, own_ref, other_ref, in_w, in_b, hid_w_hbm, hid_b, out_w, out_b, means, hid_w, copy_sems
+    )(counts, offsets, *inputs)
+
+
+def put_half(ref, half, hid_w_hbm, buffer, copy_sems):
+    scale = 1.0 / ref[COUNT_ROWS[half] : COUNT_ROWS[half] + 1, :]
+    copies = []
+    for i, (layer, side, first, rows, at) in enumerate(PIECES[half]):
+        buffer[at : at + rows, :] = ref[at : at + rows, :] * scale
+        copies.append(
+            pltpu.make_async_copy(
+                buffer.at[pl.ds(at, rows), :],
+                hid_w_hbm.at[layer, pl.ds(first, rows), pl.ds(side * 128, 128)],
+                copy_sems.at[i],
+            )
+        )
+        copies[-1].start()
+    return copies
+
+
+def own_kernel(own_ref, hid_w_hbm, buffer, copy_sems):
+    core = lax.axis_index(NEAR)
+    for half in range(2):
+
+        @pl.when(core == half)
+        def _():
+            for copy in put_half(own_ref, half, hid_w_hbm, buffer, copy_sems):
+                copy.wait()
+
+
+def other_kernel(
+    own_ref, other_ref, _, hid_w_hbm, in_w, in_b, hid_b, out_w, out_b, means, buffer, copy_sems
 ):
-    def fill(halves):
-        def rows(begin, count):
-            parts = []
-            while count:
-                which, inside = divmod(begin, HALF_ROWS)
-                taken = min(count, HALF_ROWS - inside)
-                parts.append(halves[which][inside : inside + taken, :])
-                begin, count = begin + taken, count - taken
-            return parts[0] if len(parts) == 1 else jnp.concatenate(parts, axis=0)
-
-        small = jnp.concatenate([rows(SMALL_ROW, 16), rows(SMALL_ROW + 16, 16)], axis=1)
-        scalars = small[10:11]
-        scale = 1.0 / scalars[0:1, 6:7]
-        copies = []
-        for slot in range(3):
-            hid_w[slot, :, 0:128] = rows(slot * 512, 256) * scale
-            hid_w[slot, :, 128:256] = rows(slot * 512 + 256, 256) * scale
-            copies.append(
-                pltpu.make_async_copy(hid_w.at[slot], hid_w_hbm.at[slot], copy_sems.at[slot])
-            )
-            copies[-1].start()
-        scaled = small * scale
-        hid_b[...] = scaled[0:3]
-        in_w[...] = scaled[3:6]
-        in_b[...] = scaled[6:7]
-        out_w[...] = scaled[7:10]
+    core = lax.axis_index(NEAR)
+
+    def small(ref):
+        scale = 1.0 / ref[COUNT_ROWS[1] : COUNT_ROWS[1] + 1, :]
+        left = ref[SMALL_ROW : SMALL_ROW + 16, :] * scale
+        right = ref[SMALL_ROW + 16 : SMALL_ROW + 32, :] * scale
+        rows = jnp.concatenate([left, right], axis=1)
+        hid_b[...] = rows[0:3]
+        in_w[...] = rows[3:6]
+        in_b[...] = rows[6:7]
+        out_w[...] = rows[7:10]
         for i in range(3):
-            means[i] = scaled[10, i]
-            out_b[i] = scaled[10, 3 + i]
-        for copy in copies:
-            copy.wait()
-
-    @pl.when(core_ref[0] == 0)
-    def _():
-        fill((own_ref, other_ref))
-
-    @pl.when(core_ref[0] == 1)
-    def _():
-        fill((other_ref, own_ref))
-
-
-def unpacked(core, own, other):
+            means[i] = left[10, i]
+            out_b[i] = left[10, 3 + i]
+
+    for half in range(2):
+
+        @pl.when(core == 1 - half)
+        def _():
+            copies = put_half(other_ref, half, hid_w_hbm, buffer, copy_sems)
+            small((own_ref, other_ref)[half])
+            for copy in copies:
+                copy.wait()
+
+
+def unpacked(own, other):
     vmem = pl.BlockSpec(memory_space=pltpu.VMEM)
     smem = pl.BlockSpec(memory_space=pltpu.SMEM)
-    shapes = [(3, WIDTH), (1, WIDTH), (3, WIDTH, WIDTH), (3, WIDTH), (3, WIDTH), (3,), (3,)]
-    in_w, in_b, hid_w, hid_b, out_w, out_b, means = pl.pallas_call(
-        unpack_kernel,
-        out_shape=[jax.ShapeDtypeStruct(s, F32) for s in shapes],
-        in_specs=[smem, vmem, vmem],
-        out_specs=[vmem, vmem, pl.BlockSpec(memory_space=pltpu.HBM), vmem, vmem, smem, smem],
-        scratch_shapes=[
-            pltpu.VMEM((3, WIDTH, WIDTH), F32),
-            pltpu.SemaphoreType.DMA((3,)),
-        ],
-        compiler_params=pltpu.CompilerParams(vmem_limit_bytes=8 * 1024 * 1024),
-        name="unpack",
-    )(core, own, other)
+    hbm = pl.BlockSpec(memory_space=pltpu.HBM)
+    whole = jax.ShapeDtypeStruct((3, WIDTH, WIDTH), F32)
+    scratch = [pltpu.VMEM((HALF_ROWS, 128), F32), pltpu.SemaphoreType.DMA((4,))]
+    params = pltpu.CompilerParams(vmem_limit_bytes=8 * 1024 * 1024)
+    half_done = pl.pallas_call(
+        own_kernel,
+        out_shape=whole,
+        in_specs=[vmem],
+        out_specs=hbm,
+        scratch_shapes=scratch,
+        compiler_params=params,
+        cost_estimate=pl.CostEstimate(flops=10**8, bytes_accessed=10**6, transcendentals=0),
+        name="unpack_own",
+    )(own)
+    shapes = [(3, WIDTH), (1, WIDTH), (3, WIDTH), (3, WIDTH), (3,), (3,)]
+    hid_w, in_w, in_b, hid_b, out_w, out_b, means = pl.pallas_call(
+        other_kernel,
+        out_shape=[whole] + [jax.ShapeDtypeStruct(s, F32) for s in shapes],
+        in_specs=[vmem, vmem, hbm],
+        out_specs=[hbm] + [vmem] * 4 + [smem] * 2,
+        scratch_shapes=scratch,
+        input_output_aliases={2: 0},
+        compiler_params=params,
+        name="unpack_other",
+    )(own, other, half_done)
     return in_w, in_b.reshape(WIDTH), hid_w, hid_b, out_w, out_b, means
 
 
@@ -550,9 +561,7 @@
     output_weight,
     out_bias,
 ):
-    core = lax.axis_index(NEAR).reshape(1)
     kept, given = local_terms(
-        core,
         point_counts,
         point_offsets,
         point_data,
@@ -563,7 +572,7 @@
         output_weight,
         out_bias,
     )
-    return unpacked(core, *summed_over_devices(kept, given))
+    return unpacked(*summed_over_devices(kept, given))
 
 
 def solution(mesh):

time: 74.9 us -> 73.9 us (0.987)
  Pallas kernels: 26.2 us -> 15.2 us
  starting transfers between devices: 4.71 us -> 15.4 us
  waiting for transfers between devices: 2.79 us -> 2 us
    pallas_call x2 -> x3, Pallas kernels: 26.2 us -> 15.2 us  [the longest x1 13 us: local_terms(): pl.pallas_call(step_kernel, out_shape=[half, half], in_specs=[pl.BlockSpe...]
    ppermute x1, starting transfers between devices: 1.44 us -> 12.1 us  [summed_over_devices(): mine = kept + lax.ppermute(given, NEAR, [(0, 1), (1, 0)])]
    ppermute x1, waiting for transfers between devices: 1.4 us -> 0.61 us  [summed_over_devices(): return (own, lax.ppermute(own, NEAR, [(0, 1), (1, 0)]))]
  transfers between devices with their start and end apart: 2 -> 2, of which waited for: 2 -> 2; matrix products, arithmetic and copies ran while one was open for 0% -> 0% of each run, Pallas kernels for 0% -> 1%
where the time goes in v4:
time: 73.9 us; the launch traced here: 73.6 us
  blocking collectives  38.8 us (53%)
  starting transfers between devices  15.4 us (21%)
  Pallas kernels  15.2 us (21%)
  waiting for transfers between devices  2 us (3%)
  between operations  1.96 us (3%)
    all_to_all x1, blocking collectives, summed_over_devices(): lax.all_to_all(mine.reshape(members, HALF_ROWS // members, 128), FAR, 0,...  23.3 us
    all_to_all x1, blocking collectives, summed_over_devices(): own = lax.all_to_all(spread, FAR, 0, 0, tiled=True).reshape(HALF_ROWS, 128)  15.5 us
    pallas_call x1, Pallas kernels, local_terms(): pl.pallas_call(step_kernel, out_shape=[half, half], in_specs=[pl.BlockSpe...  13 us
    ppermute x1, starting transfers between devices, summed_over_devices(): mine = kept + lax.ppermute(given, NEAR, [(0, 1), (1, 0)])  12.1 us
    ppermute x1, starting transfers between devices, summed_over_devices(): return (own, lax.ppermute(own, NEAR, [(0, 1), (1, 0)]))  3.27 us
  transfers between devices with their start and end apart: 2, of which 2 were waited for; matrix products, arithmetic and copies ran while one was open for 0% of the time, Pallas kernels for 1%

profile of v4, /device:TPU:1, one launch (start us, length us, event | category | flops | bytes accessed | tf_op | source)
XLA Modules:
  0.0 73.6 jit_solution(16225146460450189484)
XLA Ops:
  1.9 13.0 %pinn_step.1 = (f32[832,128]{1,0:T(8,128)S(1)}, f32[832,128]{1,0:T(8,128)S(1)}) custom-call(s32[1]{0:T(128)S(6)} %copy.18.counts_ref, s32[1]{0:T(128)S(6)} %copy.19.offsets_ref, f32[5,1024]{1,0:T(8,128)} %data_hbm.1, f32[3,256]{1,0:T(4,128)} %in_w_hbm.1, f32[1,256]{1,0:T(1,128)} %bitcast.2, f32[3,256,256]{2,1,0:T(8,128)} %hid_w_hbm.1, f32[3,256]{1,0:T(4,128)} %hid_b_hbm.1, ...), custom_call_target="tpu_custom_call" | custom-call | tf_op jit(solution)/shard_map/pinn_step/pallas_call | solution.py:418
  14.9 12.1 %collective-permute-start = (f32[832,128]{1,0:T(8,128)S(1)}, f32[832,128]{1,0:T(8,128)S(1)}, u32[]{:S(2)}, u32[]{:S(2)}) collective-permute-start(f32[832,128]{1,0:T(8,128)S(1)} %get-tuple-element.17), channel_id=1, source_target_pairs={{0,1},{1,0},{2,3},{3,2},{4,5},{5,4},{6,7},{7,6},{8,9},{9,8},{10,11... | collective-permute-start | bytes 1277960 | tf_op jit(solution)/shard_map/ppermute | solution.py:544
  27.0 1.4 %collective-permute-done = f32[832,128]{1,0:T(8,128)S(1)} collective-permute-done((f32[832,128]{1,0:T(8,128)S(1)}, f32[832,128]{1,0:T(8,128)S(1)}, u32[]{:S(2)}, u32[]{:S(2)}) %collective-permute-start) | collective-permute-done | bytes 426016 | tf_op jit(solution)/shard_map/ppermute | solution.py:544
  28.5 23.3 %all_to_all.10 = f32[64,13,128]{2,1,0:T(8,128)S(1)} all-to-all(f32[64,13,128]{2,1,0:T(8,128)S(1)} %reshape.28), channel_id=1, replica_groups=mesh['pts_0'=4,'pts_1'=4,'pts_2'=4,'pts_3'=2] {'pts_0','pts_1','pts_2'}, dimensions={0} | all-to-all | bytes 851968 | tf_op jit(solution)/shard_map/all_to_all | solution.py:546
  51.8 0.1 reduce_sum.9
  51.9 15.5 %all_to_all.11 = f32[64,13,128]{2,1,0:T(8,128)S(1)} all-to-all(f32[64,13,128]{2,1,0:T(8,128)S(1)} %broadcast_in_dim.2), channel_id=1, replica_groups=mesh['pts_0'=4,'pts_1'=4,'pts_2'=4,'pts_3'=2] {'pts_0','pts_1','pts_2'}, dimensions={0} | all-to-all | bytes 851968 | tf_op jit(solution)/shard_map/all_to_all | solution.py:549
  67.5 3.3 %collective-permute-start.1 = (f32[832,128]{1,0:T(8,128)S(1)}, f32[832,128]{1,0:T(8,128)S(1)}, u32[]{:S(2)}, u32[]{:S(2)}) collective-permute-start(f32[832,128]{1,0:T(8,128)S(1)} %reshape.29.own_ref), channel_id=1, source_target_pairs={{0,1},{1,0},{2,3},{3,2},{4,5},{5,4},{6,7},{7,6},{8,9},{9,8},{10,11... | collective-permute-start | bytes 1277960 | tf_op jit(solution)/shard_map/ppermute | solution.py:550
  70.8 0.8 %unpack_own.1._ = f32[3,256,256]{2,1,0:T(8,128)} custom-call(f32[832,128]{1,0:T(8,128)S(1)} %reshape.29.own_ref), custom_call_target="tpu_custom_call" | custom-call | flops 100000000 | bytes 1000000 | tf_op jit(solution)/shard_map/unpack_own/pallas_call | solution.py:519
  71.5 0.6 collective-permute-done.1.other_ref
  72.2 1.4 %unpack_other.1 = (f32[3,256,256]{2,1,0:T(8,128)}, f32[3,256]{1,0:T(4,128)}, f32[1,256]{1,0:T(1,128)}, f32[3,256]{1,0:T(4,128)}, f32[3,256]{1,0:T(4,128)}, /*index=5*/f32[3]{0:T(128)}, f32[3]{0:T(128)}) custom-call(f32[832,128]{1,0:T(8,128)S(1)} %reshape.29.own_ref, ...), custom_call_target="tpu_custom_call", output_to_operand_aliasing={{0}: (2, {})} | custom-call | tf_op jit(solution)/shard_map/unpack_other/pallas_call | solution.py:530
  (4 shorter events, 0.2 us)
Async XLA Ops:
  14.9 13.5 %collective-permute-start = (f32[832,128]{1,0:T(8,128)S(1)}, f32[832,128]{1,0:T(8,128)S(1)}, u32[]{:S(2)}, u32[]{:S(2)}) collective-permute-start(f32[832,128]{1,0:T(8,128)S(1)} %get-tuple-element.17), channel_id=1, source_target_pairs={{0,1},{1,0},{2,3},{3,2},{4,5},{5,4},{6,7},{7,6},{8,9},{9,8},{10,11... | collective-permute-start | bytes 1277960 | tf_op jit(solution)/shard_map/ppermute | solution.py:544
  67.5 4.7 %collective-permute-start.1 = (f32[832,128]{1,0:T(8,128)S(1)}, f32[832,128]{1,0:T(8,128)S(1)}, u32[]{:S(2)}, u32[]{:S(2)}) collective-permute-start(f32[832,128]{1,0:T(8,128)S(1)} %reshape.29.own_ref), channel_id=1, source_target_pairs={{0,1},{1,0},{2,3},{3,2},{4,5},{5,4},{6,7},{7,6},{8,9},{9,8},{10,11... | collective-permute-start | bytes 1277960 | tf_op jit(solution)/shard_map/ppermute | solution.py:550

commit v5 on v4

--- a/solution.py
+++ b/solution.py
@@ -143,7 +143,13 @@
     w0 = hid_w_ref[0]
     for index, w in enumerate((w0, w0 * wx, w0 * wy, hid_w_ref[1], hid_w_ref[2])):
         put_cat(w_cat, index, w)
-        put_cat(wt_cat, index, w.T)
+    for index, w in ((0, w0), (3, hid_w_ref[1]), (4, hid_w_ref[2])):
+        turned = w.T
+        put_cat(wt_cat, index, turned)
+        if index == 0:
+            for i in range(2):
+                column = cols[i]
+                put_cat(wt_cat, 1 + i, turned * jnp.concatenate([column, column], axis=1))
     out_high, out_low = split(out_w_ref[...])
     out_cat[0:3, 0:256] = out_high
     out_cat[0:3, 256:512] = out_high
@@ -540,13 +546,40 @@
     return in_w, in_b.reshape(WIDTH), hid_w, hid_b, out_w, out_b, means
 
 
+def sum_kernel(members, parts_ref, spread_ref):
+    rows = HALF_ROWS // members
+    eight = 8 * rows
+    groups = members // 8
+    total = parts_ref[0:eight, :]
+    for g in range(1, groups):
+        total = total + parts_ref[g * eight : (g + 1) * eight, :]
+    own = total[0:rows]
+    for i in range(1, 8):
+        own = own + total[i * rows : (i + 1) * rows]
+    copies = jnp.concatenate([own] * 8, axis=0)
+    for g in range(groups):
+        spread_ref[g * eight : (g + 1) * eight, :] = copies
+
+
+def sum_and_spread(parts, members):
+    vmem = pl.BlockSpec(memory_space=pltpu.VMEM)
+    return pl.pallas_call(
+        functools.partial(sum_kernel, members),
+        out_shape=jax.ShapeDtypeStruct(parts.shape, F32),
+        in_specs=[vmem],
+        out_specs=vmem,
+        compiler_params=pltpu.CompilerParams(vmem_limit_bytes=4 * 1024 * 1024),
+        name="sum_parts",
+    )(parts)
+
+
 def summed_over_devices(kept, given):
     mine = kept + lax.ppermute(given, NEAR, [(0, 1), (1, 0)])
     members = lax.axis_size(FAR)
-    parts = lax.all_to_all(mine.reshape(members, HALF_ROWS // members, 128), FAR, 0, 0, tiled=True)
-    own = parts.sum(axis=0)
-    spread = jnp.broadcast_to(own[None], (members,) + own.shape)
-    own = lax.all_to_all(spread, FAR, 0, 0, tiled=True).reshape(HALF_ROWS, 128)
+    parts = lax.all_to_all(mine.reshape(HALF_ROWS, 1, 128), FAR, 0, 0, tiled=True)
+    spread = sum_and_spread(parts.reshape(HALF_ROWS, 128), members)
+    own = lax.all_to_all(spread.reshape(HALF_ROWS, 1, 128), FAR, 0, 0, tiled=True)
+    own = own.reshape(HALF_ROWS, 128)
     return own, lax.ppermute(own, NEAR, [(0, 1), (1, 0)])
 
 

time: 73.9 us -> 71.8 us (0.972)
  blocking collectives: 38.8 us -> 37.1 us
    all_to_all x2, blocking collectives: 38.8 us -> 37.1 us  [the longest x1 22.3 us: summed_over_devices(): lax.all_to_all(mine.reshape(HALF_ROWS, 1, 128), FAR, 0, 0, tiled=True)]
where the time goes in v5:
time: 71.8 us; the launch traced here: 71.6 us
  blocking collectives  37.1 us (52%)
  starting transfers between devices  15.3 us (21%)
  Pallas kernels  15.2 us (21%)
  waiting for transfers between devices  2 us (3%)
  between operations  1.95 us (3%)
    all_to_all x1, blocking collectives, summed_over_devices(): lax.all_to_all(mine.reshape(HALF_ROWS, 1, 128), FAR, 0, 0, tiled=True)  22.3 us
    all_to_all x1, blocking collectives, summed_over_devices(): lax.all_to_all(spread.reshape(HALF_ROWS, 1, 128), FAR, 0, 0, tiled=True)  14.8 us
    pallas_call x1, Pallas kernels, local_terms(): pl.pallas_call(step_kernel, out_shape=[half, half], in_specs=[pl.BlockSpe...  12.9 us
    ppermute x1, starting transfers between devices, summed_over_devices(): mine = kept + lax.ppermute(given, NEAR, [(0, 1), (1, 0)])  12.1 us
    ppermute x1, starting transfers between devices, summed_over_devices(): return (own, lax.ppermute(own, NEAR, [(0, 1), (1, 0)]))  3.19 us
    pallas_call x1, Pallas kernels, unpacked(): pl.pallas_call(other_kernel, out_shape=[whole] + [jax.ShapeDtypeStruct(s,...  1.44 us
  transfers between devices with their start and end apart: 2, of which 2 were waited for; matrix products, arithmetic and copies ran while one was open for 0% of the time, Pallas kernels for 1%

profile of v5, /device:TPU:1, one launch (start us, length us, event | category | flops | bytes accessed | tf_op | source)
XLA Modules:
  0.0 71.6 jit_solution(7534767124925474587)
XLA Ops:
  1.9 12.9 %pinn_step.1 = (f32[832,128]{1,0:T(8,128)S(1)}, f32[832,128]{1,0:T(8,128)S(1)}) custom-call(s32[1]{0:T(128)S(6)} %copy.20.counts_ref, s32[1]{0:T(128)S(6)} %copy.21.offsets_ref, f32[5,1024]{1,0:T(8,128)} %data_hbm.1, f32[3,256]{1,0:T(4,128)} %in_w_hbm.1, f32[1,256]{1,0:T(1,128)} %bitcast.16, f32[3,256,256]{2,1,0:T(8,128)} %hid_w_hbm.1, f32[3,256]{1,0:T(4,128)} %hid_b_hbm.1, ...), custom_call_target="tpu_custom_call" | custom-call | tf_op jit(solution)/shard_map/pinn_step/pallas_call | solution.py:424
  14.9 12.1 %collective-permute-start = (f32[832,128]{1,0:T(8,128)S(1)}, f32[832,128]{1,0:T(8,128)S(1)}, u32[]{:S(2)}, u32[]{:S(2)}) collective-permute-start(f32[832,128]{1,0:T(8,128)S(1)} %get-tuple-element.17), channel_id=1, source_target_pairs={{0,1},{1,0},{2,3},{3,2},{4,5},{5,4},{6,7},{7,6},{8,9},{9,8},{10,11... | collective-permute-start | bytes 1277960 | tf_op jit(solution)/shard_map/ppermute | solution.py:577
  27.0 1.4 %collective-permute-done = f32[832,128]{1,0:T(8,128)S(1)} collective-permute-done((f32[832,128]{1,0:T(8,128)S(1)}, f32[832,128]{1,0:T(8,128)S(1)}, u32[]{:S(2)}, u32[]{:S(2)}) %collective-permute-start) | collective-permute-done | bytes 426016 | tf_op jit(solution)/shard_map/ppermute | solution.py:577
  28.4 0.1 add.3
  28.5 22.3 %all_to_all.10 = f32[832,1,128]{2,1,0:T(1,128)S(1)} all-to-all(f32[832,1,128]{2,1,0:T(1,128)S(1)} %bitcast.15), channel_id=1, replica_groups=mesh['pts_0'=4,'pts_1'=4,'pts_2'=4,'pts_3'=2] {'pts_0','pts_1','pts_2'}, dimensions={0} | all-to-all | bytes 851968 | tf_op jit(solution)/shard_map/all_to_all | solution.py:579
  50.8 0.1 sum_parts.1
  50.8 14.8 %all_to_all.11 = f32[832,1,128]{2,1,0:T(1,128)S(1)} all-to-all(f32[832,1,128]{2,1,0:T(1,128)S(1)} %bitcast.14), channel_id=1, replica_groups=mesh['pts_0'=4,'pts_1'=4,'pts_2'=4,'pts_3'=2] {'pts_0','pts_1','pts_2'}, dimensions={0} | all-to-all | bytes 851968 | tf_op jit(solution)/shard_map/all_to_all | solution.py:581
  65.6 3.2 %collective-permute-start.1 = (f32[832,128]{1,0:T(8,128)S(1)}, f32[832,128]{1,0:T(8,128)S(1)}, u32[]{:S(2)}, u32[]{:S(2)}) collective-permute-start(f32[832,128]{1,0:T(8,128)S(1)} %bitcast.10), channel_id=1, source_target_pairs={{0,1},{1,0},{2,3},{3,2},{4,5},{5,4},{6,7},{7,6},{8,9},{9,8},{10,11... | collective-permute-start | bytes 1277960 | tf_op jit(solution)/shard_map/ppermute | solution.py:583
  68.8 0.8 %unpack_own.1._ = f32[3,256,256]{2,1,0:T(8,128)} custom-call(f32[832,128]{1,0:T(8,128)S(1)} %bitcast.11), custom_call_target="tpu_custom_call" | custom-call | flops 100000000 | bytes 1000000 | tf_op jit(solution)/shard_map/unpack_own/pallas_call | solution.py:525
  69.6 0.6 collective-permute-done.1.other_ref
  70.2 1.4 %unpack_other.1 = (f32[3,256,256]{2,1,0:T(8,128)}, f32[3,256]{1,0:T(4,128)}, f32[1,256]{1,0:T(1,128)}, f32[3,256]{1,0:T(4,128)}, f32[3,256]{1,0:T(4,128)}, /*index=5*/f32[3]{0:T(128)}, f32[3]{0:T(128)}) custom-call(f32[832,128]{1,0:T(8,128)S(1)} %bitcast.12, f32[832,128]{1,0:T(8,128)S(1)} %collective-permute-done.1.other_ref, ...), custom_call_target="tpu_custom_call", output_to_operand_aliasing={{0}: (2, {})} | custom-call | tf_op jit(solution)/shard_map/unpack_other/pallas_call | solution.py:536
Async XLA Ops:
  14.9 13.5 %collective-permute-start = (f32[832,128]{1,0:T(8,128)S(1)}, f32[832,128]{1,0:T(8,128)S(1)}, u32[]{:S(2)}, u32[]{:S(2)}) collective-permute-start(f32[832,128]{1,0:T(8,128)S(1)} %get-tuple-element.17), channel_id=1, source_target_pairs={{0,1},{1,0},{2,3},{3,2},{4,5},{5,4},{6,7},{7,6},{8,9},{9,8},{10,11... | collective-permute-start | bytes 1277960 | tf_op jit(solution)/shard_map/ppermute | solution.py:577
  65.6 4.6 %collective-permute-start.1 = (f32[832,128]{1,0:T(8,128)S(1)}, f32[832,128]{1,0:T(8,128)S(1)}, u32[]{:S(2)}, u32[]{:S(2)}) collective-permute-start(f32[832,128]{1,0:T(8,128)S(1)} %bitcast.10), channel_id=1, source_target_pairs={{0,1},{1,0},{2,3},{3,2},{4,5},{5,4},{6,7},{7,6},{8,9},{9,8},{10,11... | collective-permute-start | bytes 1277960 | tf_op jit(solution)/shard_map/ppermute | solution.py:583

commit v6 on v5

--- a/solution.py
+++ b/solution.py
@@ -487,9 +487,10 @@
                 copy.wait()
 
 
-def other_kernel(
-    own_ref, other_ref, _, hid_w_hbm, in_w, in_b, hid_b, out_w, out_b, means, buffer, copy_sems
-):
+def other_kernel(own_ref, other_ref, _, hid_w_hbm, *refs):
+    small_hbm, small_refs = refs[:6], refs[6:12]
+    buffer, copy_sems, small_sems = refs[12:]
+    in_w, in_b, hid_b, out_w, out_b, means = small_refs
     core = lax.axis_index(NEAR)
 
     def small(ref):
@@ -504,20 +505,26 @@
         for i in range(3):
             means[i] = left[10, i]
             out_b[i] = left[10, 3 + i]
+        copies = [
+            pltpu.make_async_copy(source, target, small_sems.at[i])
+            for i, (source, target) in enumerate(zip(small_refs, small_hbm))
+        ]
+        for copy in copies:
+            copy.start()
+        return copies
 
     for half in range(2):
 
         @pl.when(core == 1 - half)
         def _():
             copies = put_half(other_ref, half, hid_w_hbm, buffer, copy_sems)
-            small((own_ref, other_ref)[half])
+            copies += small((own_ref, other_ref)[half])
             for copy in copies:
                 copy.wait()
 
 
 def unpacked(own, other):
     vmem = pl.BlockSpec(memory_space=pltpu.VMEM)
-    smem = pl.BlockSpec(memory_space=pltpu.SMEM)
     hbm = pl.BlockSpec(memory_space=pltpu.HBM)
     whole = jax.ShapeDtypeStruct((3, WIDTH, WIDTH), F32)
     scratch = [pltpu.VMEM((HALF_ROWS, 128), F32), pltpu.SemaphoreType.DMA((4,))]
@@ -537,8 +544,11 @@
         other_kernel,
         out_shape=[whole] + [jax.ShapeDtypeStruct(s, F32) for s in shapes],
         in_specs=[vmem, vmem, hbm],
-        out_specs=[hbm] + [vmem] * 4 + [smem] * 2,
-        scratch_shapes=scratch,
+        out_specs=[hbm] * 7,
+        scratch_shapes=[pltpu.VMEM(s, F32) for s in shapes[:4]]
+        + [pltpu.SMEM(s, F32) for s in shapes[4:]]
+        + scratch
+        + [pltpu.SemaphoreType.DMA((6,))],
         input_output_aliases={2: 0},
         compiler_params=params,
         name="unpack_other",

time: 71.8 us -> 71.3 us (level)
  starting transfers between devices: 15.3 us -> 4.63 us
  Pallas kernels: 15.2 us -> 25.4 us
    pallas_call x1, Pallas kernels: 12.9 us -> 23.6 us  [local_terms(): pl.pallas_call(step_kernel, out_shape=[half, half], in_specs=[pl.BlockSpe...]
    ppermute x1, starting transfers between devices: 12.1 us -> 1.44 us  [summed_over_devices(): mine = kept + lax.ppermute(given, NEAR, [(0, 1), (1, 0)])]
where the time goes in v6:
time: 71.3 us; the launch traced here: 71.1 us
  blocking collectives  37.1 us (52%)
  Pallas kernels  25.4 us (36%)
  starting transfers between devices  4.63 us (6%)
  waiting for transfers between devices  2 us (3%)
  between operations  1.95 us (3%)
    pallas_call x1, Pallas kernels, local_terms(): pl.pallas_call(step_kernel, out_shape=[half, half], in_specs=[pl.BlockSpe...  23.6 us
    all_to_all x1, blocking collectives, summed_over_devices(): lax.all_to_all(mine.reshape(HALF_ROWS, 1, 128), FAR, 0, 0, tiled=True)  22.3 us
    all_to_all x1, blocking collectives, summed_over_devices(): lax.all_to_all(spread.reshape(HALF_ROWS, 1, 128), FAR, 0, 0, tiled=True)  14.8 us
    ppermute x1, starting transfers between devices, summed_over_devices(): return (own, lax.ppermute(own, NEAR, [(0, 1), (1, 0)]))  3.19 us
    ppermute x1, starting transfers between devices, summed_over_devices(): mine = kept + lax.ppermute(given, NEAR, [(0, 1), (1, 0)])  1.44 us
  transfers between devices with their start and end apart: 2, of which 2 were waited for; matrix products, arithmetic and copies ran while one was open for 0% of the time, Pallas kernels for 1%

profile of v6, /device:TPU:1, one launch (start us, length us, event | category | flops | bytes accessed | tf_op | source)
XLA Modules:
  0.0 71.1 jit_solution(14481886862425313278)
XLA Ops:
  1.9 23.6 %pinn_step.1 = (f32[832,128]{1,0:T(8,128)S(1)}, f32[832,128]{1,0:T(8,128)S(1)}) custom-call(s32[1]{0:T(128)S(6)} %copy.20.counts_ref, s32[1]{0:T(128)S(6)} %copy.21.offsets_ref, f32[5,1024]{1,0:T(8,128)} %data_hbm.1, f32[3,256]{1,0:T(4,128)} %in_w_hbm.1, f32[1,256]{1,0:T(1,128)} %bitcast.16, f32[3,256,256]{2,1,0:T(8,128)} %hid_w_hbm.1, f32[3,256]{1,0:T(4,128)} %hid_b_hbm.1, ...), custom_call_target="tpu_custom_call" | custom-call | tf_op jit(solution)/shard_map/pinn_step/pallas_call | solution.py:424
  25.6 1.4 %collective-permute-start = (f32[832,128]{1,0:T(8,128)S(1)}, f32[832,128]{1,0:T(8,128)S(1)}, u32[]{:S(2)}, u32[]{:S(2)}) collective-permute-start(f32[832,128]{1,0:T(8,128)S(1)} %get-tuple-element.17), channel_id=1, source_target_pairs={{0,1},{1,0},{2,3},{3,2},{4,5},{5,4},{6,7},{7,6},{8,9},{9,8},{10,11... | collective-permute-start | bytes 1277960 | tf_op jit(solution)/shard_map/ppermute | solution.py:587
  27.0 1.4 %collective-permute-done = f32[832,128]{1,0:T(8,128)S(1)} collective-permute-done((f32[832,128]{1,0:T(8,128)S(1)}, f32[832,128]{1,0:T(8,128)S(1)}, u32[]{:S(2)}, u32[]{:S(2)}) %collective-permute-start) | collective-permute-done | bytes 426016 | tf_op jit(solution)/shard_map/ppermute | solution.py:587
  28.4 0.1 add.3
  28.5 22.3 %all_to_all.10 = f32[832,1,128]{2,1,0:T(1,128)S(1)} all-to-all(f32[832,1,128]{2,1,0:T(1,128)S(1)} %bitcast.15), channel_id=1, replica_groups=mesh['pts_0'=4,'pts_1'=4,'pts_2'=4,'pts_3'=2] {'pts_0','pts_1','pts_2'}, dimensions={0} | all-to-all | bytes 851968 | tf_op jit(solution)/shard_map/all_to_all | solution.py:589
  50.8 0.1 sum_parts.1
  50.8 14.8 %all_to_all.11 = f32[832,1,128]{2,1,0:T(1,128)S(1)} all-to-all(f32[832,1,128]{2,1,0:T(1,128)S(1)} %bitcast.14), channel_id=1, replica_groups=mesh['pts_0'=4,'pts_1'=4,'pts_2'=4,'pts_3'=2] {'pts_0','pts_1','pts_2'}, dimensions={0} | all-to-all | bytes 851968 | tf_op jit(solution)/shard_map/all_to_all | solution.py:591
  65.6 3.2 %collective-permute-start.1 = (f32[832,128]{1,0:T(8,128)S(1)}, f32[832,128]{1,0:T(8,128)S(1)}, u32[]{:S(2)}, u32[]{:S(2)}) collective-permute-start(f32[832,128]{1,0:T(8,128)S(1)} %bitcast.10), channel_id=1, source_target_pairs={{0,1},{1,0},{2,3},{3,2},{4,5},{5,4},{6,7},{7,6},{8,9},{9,8},{10,11... | collective-permute-start | bytes 1277960 | tf_op jit(solution)/shard_map/ppermute | solution.py:593
  68.8 0.8 %unpack_own.1._ = f32[3,256,256]{2,1,0:T(8,128)} custom-call(f32[832,128]{1,0:T(8,128)S(1)} %bitcast.11), custom_call_target="tpu_custom_call" | custom-call | flops 100000000 | bytes 1000000 | tf_op jit(solution)/shard_map/unpack_own/pallas_call | solution.py:532
  69.6 0.6 collective-permute-done.1.other_ref
  70.2 0.9 %unpack_other.1 = (f32[3,256,256]{2,1,0:T(8,128)}, f32[3,256]{1,0:T(4,128)}, f32[1,256]{1,0:T(1,128)}, f32[3,256]{1,0:T(4,128)}, f32[3,256]{1,0:T(4,128)}, /*index=5*/f32[3]{0:T(128)}, f32[3]{0:T(128)}) custom-call(f32[832,128]{1,0:T(8,128)S(1)} %bitcast.12, f32[832,128]{1,0:T(8,128)S(1)} %collective-permute-done.1.other_ref, ...), custom_call_target="tpu_custom_call", output_to_operand_aliasing={{0}: (2, {})} | custom-call | tf_op jit(solution)/shard_map/unpack_other/pallas_call | solution.py:543
Async XLA Ops:
  25.6 2.8 %collective-permute-start = (f32[832,128]{1,0:T(8,128)S(1)}, f32[832,128]{1,0:T(8,128)S(1)}, u32[]{:S(2)}, u32[]{:S(2)}) collective-permute-start(f32[832,128]{1,0:T(8,128)S(1)} %get-tuple-element.17), channel_id=1, source_target_pairs={{0,1},{1,0},{2,3},{3,2},{4,5},{5,4},{6,7},{7,6},{8,9},{9,8},{10,11... | collective-permute-start | bytes 1277960 | tf_op jit(solution)/shard_map/ppermute | solution.py:587
  65.6 4.6 %collective-permute-start.1 = (f32[832,128]{1,0:T(8,128)S(1)}, f32[832,128]{1,0:T(8,128)S(1)}, u32[]{:S(2)}, u32[]{:S(2)}) collective-permute-start(f32[832,128]{1,0:T(8,128)S(1)} %bitcast.10), channel_id=1, source_target_pairs={{0,1},{1,0},{2,3},{3,2},{4,5},{5,4},{6,7},{7,6},{8,9},{9,8},{10,11... | collective-permute-start | bytes 1277960 | tf_op jit(solution)/shard_map/ppermute | solution.py:593

commit v7 on v6

--- a/solution.py
+++ b/solution.py
@@ -15,7 +15,7 @@
 VISCOSITY = 0.2
 HALF = 256
 WIDTH = 256
-ROWS = 16
+ROWS = 32
 F32 = jnp.float32
 BF16 = jnp.bfloat16
 JETS = 4
@@ -170,7 +170,7 @@
 
         def row(i, lane):
             tile = rows_buf[at, i, :, lane]
-            return jnp.concatenate([tile, tile], axis=0)
+            return jnp.concatenate([tile] * (ROWS // 8), axis=0)
 
         for i in range(3):
             spread(i, points[i : i + 1, :])

time: 71.3 us -> 71.2 us (level)
  no operation moved by 1% of the time
where the time goes in v7:
time: 71.2 us; the launch traced here: 71.1 us
  blocking collectives  37.1 us (52%)
  Pallas kernels  25.4 us (36%)
  starting transfers between devices  4.63 us (7%)
  waiting for transfers between devices  2 us (3%)
  between operations  1.95 us (3%)
    pallas_call x1, Pallas kernels, local_terms(): pl.pallas_call(step_kernel, out_shape=[half, half], in_specs=[pl.BlockSpe...  23.6 us
    all_to_all x1, blocking collectives, summed_over_devices(): lax.all_to_all(mine.reshape(HALF_ROWS, 1, 128), FAR, 0, 0, tiled=True)  22.3 us
    all_to_all x1, blocking collectives, summed_over_devices(): lax.all_to_all(spread.reshape(HALF_ROWS, 1, 128), FAR, 0, 0, tiled=True)  14.8 us
    ppermute x1, starting transfers between devices, summed_over_devices(): return (own, lax.ppermute(own, NEAR, [(0, 1), (1, 0)]))  3.19 us
    ppermute x1, starting transfers between devices, summed_over_devices(): mine = kept + lax.ppermute(given, NEAR, [(0, 1), (1, 0)])  1.44 us
  transfers between devices with their start and end apart: 2, of which 2 were waited for; matrix products, arithmetic and copies ran while one was open for 0% of the time, Pallas kernels for 1%

profile of v7, /device:TPU:1, one launch (start us, length us, event | category | flops | bytes accessed | tf_op | source)
XLA Modules:
  0.0 71.1 jit_solution(14481886862425313278)
XLA Ops:
  1.9 23.6 %pinn_step.1 = (f32[832,128]{1,0:T(8,128)S(1)}, f32[832,128]{1,0:T(8,128)S(1)}) custom-call(s32[1]{0:T(128)S(6)} %copy.20.counts_ref, s32[1]{0:T(128)S(6)} %copy.21.offsets_ref, f32[5,1024]{1,0:T(8,128)} %data_hbm.1, f32[3,256]{1,0:T(4,128)} %in_w_hbm.1, f32[1,256]{1,0:T(1,128)} %bitcast.16, f32[3,256,256]{2,1,0:T(8,128)} %hid_w_hbm.1, f32[3,256]{1,0:T(4,128)} %hid_b_hbm.1, ...), custom_call_target="tpu_custom_call" | custom-call | tf_op jit(solution)/shard_map/pinn_step/pallas_call | solution.py:424
  25.6 1.4 %collective-permute-start = (f32[832,128]{1,0:T(8,128)S(1)}, f32[832,128]{1,0:T(8,128)S(1)}, u32[]{:S(2)}, u32[]{:S(2)}) collective-permute-start(f32[832,128]{1,0:T(8,128)S(1)} %get-tuple-element.17), channel_id=1, source_target_pairs={{0,1},{1,0},{2,3},{3,2},{4,5},{5,4},{6,7},{7,6},{8,9},{9,8},{10,11... | collective-permute-start | bytes 1277960 | tf_op jit(solution)/shard_map/ppermute | solution.py:587
  27.0 1.4 %collective-permute-done = f32[832,128]{1,0:T(8,128)S(1)} collective-permute-done((f32[832,128]{1,0:T(8,128)S(1)}, f32[832,128]{1,0:T(8,128)S(1)}, u32[]{:S(2)}, u32[]{:S(2)}) %collective-permute-start) | collective-permute-done | bytes 426016 | tf_op jit(solution)/shard_map/ppermute | solution.py:587
  28.4 0.1 add.3
  28.5 22.3 %all_to_all.10 = f32[832,1,128]{2,1,0:T(1,128)S(1)} all-to-all(f32[832,1,128]{2,1,0:T(1,128)S(1)} %bitcast.15), channel_id=1, replica_groups=mesh['pts_0'=4,'pts_1'=4,'pts_2'=4,'pts_3'=2] {'pts_0','pts_1','pts_2'}, dimensions={0} | all-to-all | bytes 851968 | tf_op jit(solution)/shard_map/all_to_all | solution.py:589
  50.8 0.1 sum_parts.1
  50.8 14.8 %all_to_all.11 = f32[832,1,128]{2,1,0:T(1,128)S(1)} all-to-all(f32[832,1,128]{2,1,0:T(1,128)S(1)} %bitcast.14), channel_id=1, replica_groups=mesh['pts_0'=4,'pts_1'=4,'pts_2'=4,'pts_3'=2] {'pts_0','pts_1','pts_2'}, dimensions={0} | all-to-all | bytes 851968 | tf_op jit(solution)/shard_map/all_to_all | solution.py:591
  65.6 3.2 %collective-permute-start.1 = (f32[832,128]{1,0:T(8,128)S(1)}, f32[832,128]{1,0:T(8,128)S(1)}, u32[]{:S(2)}, u32[]{:S(2)}) collective-permute-start(f32[832,128]{1,0:T(8,128)S(1)} %bitcast.10), channel_id=1, source_target_pairs={{0,1},{1,0},{2,3},{3,2},{4,5},{5,4},{6,7},{7,6},{8,9},{9,8},{10,11... | collective-permute-start | bytes 1277960 | tf_op jit(solution)/shard_map/ppermute | solution.py:593
  68.8 0.8 %unpack_own.1._ = f32[3,256,256]{2,1,0:T(8,128)} custom-call(f32[832,128]{1,0:T(8,128)S(1)} %bitcast.11), custom_call_target="tpu_custom_call" | custom-call | flops 100000000 | bytes 1000000 | tf_op jit(solution)/shard_map/unpack_own/pallas_call | solution.py:532
  69.6 0.6 collective-permute-done.1.other_ref
  70.2 0.9 %unpack_other.1 = (f32[3,256,256]{2,1,0:T(8,128)}, f32[3,256]{1,0:T(4,128)}, f32[1,256]{1,0:T(1,128)}, f32[3,256]{1,0:T(4,128)}, f32[3,256]{1,0:T(4,128)}, /*index=5*/f32[3]{0:T(128)}, f32[3]{0:T(128)}) custom-call(f32[832,128]{1,0:T(8,128)S(1)} %bitcast.12, f32[832,128]{1,0:T(8,128)S(1)} %collective-permute-done.1.other_ref, ...), custom_call_target="tpu_custom_call", output_to_operand_aliasing={{0}: (2, {})} | custom-call | tf_op jit(solution)/shard_map/unpack_other/pallas_call | solution.py:543
Async XLA Ops:
  25.6 2.8 %collective-permute-start = (f32[832,128]{1,0:T(8,128)S(1)}, f32[832,128]{1,0:T(8,128)S(1)}, u32[]{:S(2)}, u32[]{:S(2)}) collective-permute-start(f32[832,128]{1,0:T(8,128)S(1)} %get-tuple-element.17), channel_id=1, source_target_pairs={{0,1},{1,0},{2,3},{3,2},{4,5},{5,4},{6,7},{7,6},{8,9},{9,8},{10,11... | collective-permute-start | bytes 1277960 | tf_op jit(solution)/shard_map/ppermute | solution.py:587
  65.6 4.6 %collective-permute-start.1 = (f32[832,128]{1,0:T(8,128)S(1)}, f32[832,128]{1,0:T(8,128)S(1)}, u32[]{:S(2)}, u32[]{:S(2)}) collective-permute-start(f32[832,128]{1,0:T(8,128)S(1)} %bitcast.10), channel_id=1, source_target_pairs={{0,1},{1,0},{2,3},{3,2},{4,5},{5,4},{6,7},{7,6},{8,9},{9,8},{10,11... | collective-permute-start | bytes 1277960 | tf_op jit(solution)/shard_map/ppermute | solution.py:593
